TPU v7x, 8 devices: a whole 2x2x1 slice. The times are simulated.
8 devices in a mesh: dp: 1 (over z), fsdp: 8 (over y, x, core).
Axes of the slice: x: 2, y: 2, z: 1, core: 2. Of those that a mesh axis runs over, the one named last changes fastest.
Arguments:
- hidden: bfloat16 [8192, 512], P(('dp', 'fsdp'))
- targets: int32 [8192], P(('dp', 'fsdp'))
- weight: bfloat16 [32128, 512], P('fsdp')
Outputs:
- output 1: float32 [1], P('dp')
- output 2: float32 [8192, 512], P(('dp', 'fsdp'))
- output 3: float32 [32128, 512], P(('dp', 'fsdp'))
All inputs are finite; a program needn't handle non-finite values.
Results may differ from a plain program's by a relative error of at most 0.001.
Values are sent between devices in bfloat16 or wider.
A program may use at most 1 GiB of HBM per device.

v0:
```python
import jax
import jax.numpy as jnp
from jax import lax
from jax.sharding import PartitionSpec as P


def solution(mesh):
    groups = mesh.shape["fsdp"]
    ring_pairs = [(src_idx, (src_idx + 1) % groups) for src_idx in range(groups)]
    tok_spec = P(("dp", "fsdp"), None)

    def local_head(hidden, targets, weight):
        tok_loc = hidden.shape[0]
        shard_rows = weight.shape[0]
        tokens = tok_loc * groups
        rank_id = lax.axis_index("fsdp")
        col_ids = jnp.arange(shard_rows, dtype=jnp.int32)

        def block_logits(w_blk, step_idx):
            owner_idx = (rank_id - step_idx) % groups
            logits = lax.dot_general(hidden, w_blk, (((1,), (1,)), ((), ())), preferred_element_type=jnp.float32)
            is_target = (targets - owner_idx * shard_rows)[:, None] == col_ids[None, :]
            return logits, is_target

        def fwd_update(fwd_state, w_blk, step_idx):
            run_max, run_sum, tgt_logit = fwd_state
            logits, is_target = block_logits(w_blk, step_idx)
            new_max = jnp.maximum(run_max, jnp.max(logits, axis=1))
            run_sum = run_sum * jnp.exp(run_max - new_max) + jnp.sum(jnp.exp(logits - new_max[:, None]), axis=1)
            tgt_logit = tgt_logit + jnp.sum(jnp.where(is_target, logits, 0.0), axis=1)
            return new_max, run_sum, tgt_logit

        def fwd_body(step_idx, loop_state):
            w_cur, fwd_state = loop_state
            w_cur = lax.ppermute(w_cur, "fsdp", ring_pairs)
            return w_cur, fwd_update(fwd_state, w_cur, step_idx)

        init_state = (jnp.full((tok_loc,), -jnp.inf, jnp.float32), jnp.zeros((tok_loc,), jnp.float32), jnp.zeros((tok_loc,), jnp.float32))
        first_state = fwd_update(init_state, weight, 0)
        run_max, run_sum, tgt_logit = lax.fori_loop(1, groups, fwd_body, (weight, first_state))[1]
        log_norm = run_max + jnp.log(run_sum)
        loss_val = lax.psum(jnp.sum(log_norm - tgt_logit) / tokens, "fsdp").reshape(1)

        def bwd_update(w_blk, step_idx):
            logits, is_target = block_logits(w_blk, step_idx)
            dlogits = ((jnp.exp(logits - log_norm[:, None]) - is_target.astype(jnp.float32)) / tokens).astype(jnp.bfloat16)
            dh_part = jnp.dot(dlogits, w_blk, preferred_element_type=jnp.float32)
            dw_part = lax.dot_general(dlogits, hidden, (((0,), (0,)), ((), ())), preferred_element_type=jnp.float32)
            return dh_part, dw_part

        def bwd_body(step_idx, loop_state):
            w_cur, dw_acc, grad_h = loop_state
            w_cur = lax.ppermute(w_cur, "fsdp", ring_pairs)
            dw_acc = lax.ppermute(dw_acc, "fsdp", ring_pairs)
            dh_part, dw_part = bwd_update(w_cur, step_idx)
            return w_cur, dw_acc + dw_part, grad_h + dh_part

        grad_h, dw_acc = bwd_update(weight, 0)
        final_state = lax.fori_loop(1, groups, bwd_body, (weight, dw_acc, grad_h))
        grad_w = lax.ppermute(final_state[1], "fsdp", ring_pairs)
        return loss_val, final_state[2], grad_w

    return jax.shard_map(local_head, mesh=mesh, in_specs=(tok_spec, P(("dp", "fsdp")), P("fsdp", None)), out_specs=(P("dp"), tok_spec, tok_spec), check_vma=False)
```

profile of v0, /device:TPU:0, one launch (start us, length us, event | category | flops | bytes accessed | tf_op | source)
XLA Modules:
  0.0 1759.4 jit_solution(5374391465046401774)
XLA Ops:
  0.6 4.4 copy.35
  5.1 4.6 copy.7
  9.7 8.0 fusion.7
  17.7 8.0 select_reduce_fusion.1
  25.7 443.1 %while.42 = (s32[]{:T(128)}, bf16[4016,512]{1,0:T(8,128)(2,1)}, f32[1024]{0:T(1024)S(1)}, f32[1024]{0:T(1024)S(1)}, f32[1024]{0:T(1024)S(1)}, /*index=5*/bf16[10...) while((s32[]{:T(128)}, bf16[4016,512]{1,0:T(8,128)(2,1)}, ...), condition=%wide.region_7.8_spmd.clone, body=%wide.region_3.7_spmd.clone.sunk | while | flops 4235758592 | bytes 62816552 | solution.py:40
  26.6 48.2 %collective-permute-done = bf16[4016,512]{1,0:T(8,128)(2,1)} collective-permute-done((bf16[4016,512]{1,0:T(8,128)(2,1)}, bf16[4016,512]{1,0:T(8,128)(2,1)}, u32[]{:S(2)}, u32[]{:S(2)}) %collective-permute-start) | collective-permute-done | bytes 4112416 | tf_op jit(solution)/shard_map/while/body/eval_jaxpr/ppermute | solution.py:35
  74.7 6.4 fusion.31
  85.5 4.4 copy.17
  89.9 47.9 %collective-permute-done = bf16[4016,512]{1,0:T(8,128)(2,1)} collective-permute-done((bf16[4016,512]{1,0:T(8,128)(2,1)}, bf16[4016,512]{1,0:T(8,128)(2,1)}, u32[]{:S(2)}, u32[]{:S(2)}) %collective-permute-start) | collective-permute-done | bytes 4112416 | tf_op jit(solution)/shard_map/while/body/eval_jaxpr/ppermute | solution.py:35
  137.9 6.4 fusion.31
  148.7 4.4 copy.17
  153.1 47.9 %collective-permute-done = bf16[4016,512]{1,0:T(8,128)(2,1)} collective-permute-done((bf16[4016,512]{1,0:T(8,128)(2,1)}, bf16[4016,512]{1,0:T(8,128)(2,1)}, u32[]{:S(2)}, u32[]{:S(2)}) %collective-permute-start) | collective-permute-done | bytes 4112416 | tf_op jit(solution)/shard_map/while/body/eval_jaxpr/ppermute | solution.py:35
  201.0 6.4 fusion.31
  211.8 4.4 copy.17
  216.2 47.9 %collective-permute-done = bf16[4016,512]{1,0:T(8,128)(2,1)} collective-permute-done((bf16[4016,512]{1,0:T(8,128)(2,1)}, bf16[4016,512]{1,0:T(8,128)(2,1)}, u32[]{:S(2)}, u32[]{:S(2)}) %collective-permute-start) | collective-permute-done | bytes 4112416 | tf_op jit(solution)/shard_map/while/body/eval_jaxpr/ppermute | solution.py:35
  264.2 6.4 fusion.31
  274.9 4.4 copy.17
  279.4 47.9 %collective-permute-done = bf16[4016,512]{1,0:T(8,128)(2,1)} collective-permute-done((bf16[4016,512]{1,0:T(8,128)(2,1)}, bf16[4016,512]{1,0:T(8,128)(2,1)}, u32[]{:S(2)}, u32[]{:S(2)}) %collective-permute-start) | collective-permute-done | bytes 4112416 | tf_op jit(solution)/shard_map/while/body/eval_jaxpr/ppermute | solution.py:35
  327.3 6.4 fusion.31
  338.1 4.4 copy.17
  342.5 47.9 %collective-permute-done = bf16[4016,512]{1,0:T(8,128)(2,1)} collective-permute-done((bf16[4016,512]{1,0:T(8,128)(2,1)}, bf16[4016,512]{1,0:T(8,128)(2,1)}, u32[]{:S(2)}, u32[]{:S(2)}) %collective-permute-start) | collective-permute-done | bytes 4112416 | tf_op jit(solution)/shard_map/while/body/eval_jaxpr/ppermute | solution.py:35
  390.4 6.4 fusion.31
  401.2 4.4 copy.17
  405.6 47.9 %collective-permute-done = bf16[4016,512]{1,0:T(8,128)(2,1)} collective-permute-done((bf16[4016,512]{1,0:T(8,128)(2,1)}, bf16[4016,512]{1,0:T(8,128)(2,1)}, u32[]{:S(2)}, u32[]{:S(2)}) %collective-permute-start) | collective-permute-done | bytes 4112416 | tf_op jit(solution)/shard_map/while/body/eval_jaxpr/ppermute | solution.py:35
  453.6 6.4 fusion.31
  464.4 4.4 copy.17
  469.4 9.5 fusion.4
  480.9 7.5 fusion.5
  488.4 1155.0 %while.43 = (s32[]{:T(128)}, bf16[4016,512]{1,0:T(8,128)(2,1)}, f32[4016,512]{1,0:T(8,128)}, f32[1024,512]{1,0:T(8,128)S(1)}, bf16[1024,512]{1,0:T(8,128)(2,1)S(...) while((s32[]{:T(128)}, bf16[4016,512]{1,0:T(8,128)(2,1)}, ...), condition=%wide.region_11.12_spmd.clone, body=%wide.region_10.11_spmd.clone.sunk | while | flops 12660499456 | bytes 113230160 | solution.py:59
  488.4 136.1 %collective-permute-done.1 = bf16[4016,512]{1,0:T(8,128)(2,1)} collective-permute-done((bf16[4016,512]{1,0:T(8,128)(2,1)}, bf16[4016,512]{1,0:T(8,128)(2,1)}, u32[]{:S(2)}, u32[]{:S(2)}) %collective-permute-start.1) | collective-permute-done | bytes 4112416 | tf_op jit(solution)/shard_map/while/body/eval_jaxpr/ppermute | solution.py:53
  624.5 4.4 copy.30
  628.8 9.2 multiply_convert_fusion.5
  638.1 6.5 convolution_add_fusion.5
  644.6 8.8 convolution_add_fusion.4
  653.4 136.1 %collective-permute-done.1 = bf16[4016,512]{1,0:T(8,128)(2,1)} collective-permute-done((bf16[4016,512]{1,0:T(8,128)(2,1)}, bf16[4016,512]{1,0:T(8,128)(2,1)}, u32[]{:S(2)}, u32[]{:S(2)}) %collective-permute-start.1) | collective-permute-done | bytes 4112416 | tf_op jit(solution)/shard_map/while/body/eval_jaxpr/ppermute | solution.py:53
  789.5 4.4 copy.30
  793.8 9.2 multiply_convert_fusion.5
  803.1 6.5 convolution_add_fusion.5
  809.6 8.8 convolution_add_fusion.4
  818.4 136.1 %collective-permute-done.1 = bf16[4016,512]{1,0:T(8,128)(2,1)} collective-permute-done((bf16[4016,512]{1,0:T(8,128)(2,1)}, bf16[4016,512]{1,0:T(8,128)(2,1)}, u32[]{:S(2)}, u32[]{:S(2)}) %collective-permute-start.1) | collective-permute-done | bytes 4112416 | tf_op jit(solution)/shard_map/while/body/eval_jaxpr/ppermute | solution.py:53
  954.5 4.4 copy.30
  958.8 9.2 multiply_convert_fusion.5
  968.1 6.5 convolution_add_fusion.5
  974.6 8.8 convolution_add_fusion.4
  983.4 136.1 %collective-permute-done.1 = bf16[4016,512]{1,0:T(8,128)(2,1)} collective-permute-done((bf16[4016,512]{1,0:T(8,128)(2,1)}, bf16[4016,512]{1,0:T(8,128)(2,1)}, u32[]{:S(2)}, u32[]{:S(2)}) %collective-permute-start.1) | collective-permute-done | bytes 4112416 | tf_op jit(solution)/shard_map/while/body/eval_jaxpr/ppermute | solution.py:53
  1119.5 4.4 copy.30
  1123.8 9.2 multiply_convert_fusion.5
  1133.1 6.5 convolution_add_fusion.5
  1139.6 8.8 convolution_add_fusion.4
  1148.4 136.1 %collective-permute-done.1 = bf16[4016,512]{1,0:T(8,128)(2,1)} collective-permute-done((bf16[4016,512]{1,0:T(8,128)(2,1)}, bf16[4016,512]{1,0:T(8,128)(2,1)}, u32[]{:S(2)}, u32[]{:S(2)}) %collective-permute-start.1) | collective-permute-done | bytes 4112416 | tf_op jit(solution)/shard_map/while/body/eval_jaxpr/ppermute | solution.py:53
  1284.5 4.4 copy.30
  1288.8 9.2 multiply_convert_fusion.5
  1298.1 6.5 convolution_add_fusion.5
  1304.6 8.8 convolution_add_fusion.4
  1313.4 136.1 %collective-permute-done.1 = bf16[4016,512]{1,0:T(8,128)(2,1)} collective-permute-done((bf16[4016,512]{1,0:T(8,128)(2,1)}, bf16[4016,512]{1,0:T(8,128)(2,1)}, u32[]{:S(2)}, u32[]{:S(2)}) %collective-permute-start.1) | collective-permute-done | bytes 4112416 | tf_op jit(solution)/shard_map/while/body/eval_jaxpr/ppermute | solution.py:53
  1453.8 9.2 multiply_convert_fusion.5
  1463.1 6.5 convolution_add_fusion.5
  1469.6 8.8 convolution_add_fusion.4
  1478.4 136.1 %collective-permute-done.1 = bf16[4016,512]{1,0:T(8,128)(2,1)} collective-permute-done((bf16[4016,512]{1,0:T(8,128)(2,1)}, bf16[4016,512]{1,0:T(8,128)(2,1)}, u32[]{:S(2)}, u32[]{:S(2)}) %collective-permute-start.1) | collective-permute-done | bytes 4112416 | tf_op jit(solution)/shard_map/while/body/eval_jaxpr/ppermute | solution.py:53
  1618.8 9.2 multiply_convert_fusion.5
  1628.1 6.5 convolution_add_fusion.5
  1634.6 8.8 convolution_add_fusion.4
  1644.1 107.7 %psum.7 = f32[1]{0:T(128)} all-reduce(f32[1]{0:T(128)} %bitcast), channel_id=1, replica_groups=mesh['dp'=1,'fsdp'=8] {'fsdp'}, use_global_device_ids=true, to_apply=%region_9.10 | all-reduce | flops 1 | bytes 8 | tf_op jit(solution)/shard_map/psum | solution.py:42
  1751.8 7.6 copy.36
  (94 shorter events, 42.9 us)
Async XLA Ops:
  0.6 9.0 copy-start.3
  5.1 4.6 copy-start.1
  9.7 8.0 copy-start.2
  25.7 49.1 %collective-permute-start = (bf16[4016,512]{1,0:T(8,128)(2,1)}, bf16[4016,512]{1,0:T(8,128)(2,1)}, u32[]{:S(2)}, u32[]{:S(2)}) collective-permute-start(bf16[4016,512]{1,0:T(8,128)(2,1)} %get-tuple-element.651), channel_id=1, source_target_pairs={{0,1},{1,2},{2,3},{3,4},{4,5},{5,6},{6,7},{7,0}} | collective-permute-start | bytes 12337160 | tf_op jit(solution)/shard_map/while/body/eval_jaxpr/ppermute | solution.py:35
  89.9 48.0 %collective-permute-start = (bf16[4016,512]{1,0:T(8,128)(2,1)}, bf16[4016,512]{1,0:T(8,128)(2,1)}, u32[]{:S(2)}, u32[]{:S(2)}) collective-permute-start(bf16[4016,512]{1,0:T(8,128)(2,1)} %get-tuple-element.651), channel_id=1, source_target_pairs={{0,1},{1,2},{2,3},{3,4},{4,5},{5,6},{6,7},{7,0}} | collective-permute-start | bytes 12337160 | tf_op jit(solution)/shard_map/while/body/eval_jaxpr/ppermute | solution.py:35
  153.1 48.0 %collective-permute-start = (bf16[4016,512]{1,0:T(8,128)(2,1)}, bf16[4016,512]{1,0:T(8,128)(2,1)}, u32[]{:S(2)}, u32[]{:S(2)}) collective-permute-start(bf16[4016,512]{1,0:T(8,128)(2,1)} %get-tuple-element.651), channel_id=1, source_target_pairs={{0,1},{1,2},{2,3},{3,4},{4,5},{5,6},{6,7},{7,0}} | collective-permute-start | bytes 12337160 | tf_op jit(solution)/shard_map/while/body/eval_jaxpr/ppermute | solution.py:35
  216.2 48.0 %collective-permute-start = (bf16[4016,512]{1,0:T(8,128)(2,1)}, bf16[4016,512]{1,0:T(8,128)(2,1)}, u32[]{:S(2)}, u32[]{:S(2)}) collective-permute-start(bf16[4016,512]{1,0:T(8,128)(2,1)} %get-tuple-element.651), channel_id=1, source_target_pairs={{0,1},{1,2},{2,3},{3,4},{4,5},{5,6},{6,7},{7,0}} | collective-permute-start | bytes 12337160 | tf_op jit(solution)/shard_map/while/body/eval_jaxpr/ppermute | solution.py:35
  279.4 48.0 %collective-permute-start = (bf16[4016,512]{1,0:T(8,128)(2,1)}, bf16[4016,512]{1,0:T(8,128)(2,1)}, u32[]{:S(2)}, u32[]{:S(2)}) collective-permute-start(bf16[4016,512]{1,0:T(8,128)(2,1)} %get-tuple-element.651), channel_id=1, source_target_pairs={{0,1},{1,2},{2,3},{3,4},{4,5},{5,6},{6,7},{7,0}} | collective-permute-start | bytes 12337160 | tf_op jit(solution)/shard_map/while/body/eval_jaxpr/ppermute | solution.py:35
  342.5 48.0 %collective-permute-start = (bf16[4016,512]{1,0:T(8,128)(2,1)}, bf16[4016,512]{1,0:T(8,128)(2,1)}, u32[]{:S(2)}, u32[]{:S(2)}) collective-permute-start(bf16[4016,512]{1,0:T(8,128)(2,1)} %get-tuple-element.651), channel_id=1, source_target_pairs={{0,1},{1,2},{2,3},{3,4},{4,5},{5,6},{6,7},{7,0}} | collective-permute-start | bytes 12337160 | tf_op jit(solution)/shard_map/while/body/eval_jaxpr/ppermute | solution.py:35
  405.6 48.0 %collective-permute-start = (bf16[4016,512]{1,0:T(8,128)(2,1)}, bf16[4016,512]{1,0:T(8,128)(2,1)}, u32[]{:S(2)}, u32[]{:S(2)}) collective-permute-start(bf16[4016,512]{1,0:T(8,128)(2,1)} %get-tuple-element.651), channel_id=1, source_target_pairs={{0,1},{1,2},{2,3},{3,4},{4,5},{5,6},{6,7},{7,0}} | collective-permute-start | bytes 12337160 | tf_op jit(solution)/shard_map/while/body/eval_jaxpr/ppermute | solution.py:35
  469.4 11.5 copy-start
  488.4 156.2 %collective-permute-start.2 = (f32[4016,512]{1,0:T(8,128)}, f32[4016,512]{1,0:T(8,128)}, u32[]{:S(2)}, u32[]{:S(2)}) collective-permute-start(f32[4016,512]{1,0:T(8,128)} %get-tuple-element.691), channel_id=1, source_target_pairs={{0,1},{1,2},{2,3},{3,4},{4,5},{5,6},{6,7},{7,0}} | collective-permute-start | bytes 24674312 | tf_op jit(solution)/shard_map/while/body/eval_jaxpr/ppermute | solution.py:54
  488.4 136.1 %collective-permute-start.1 = (bf16[4016,512]{1,0:T(8,128)(2,1)}, bf16[4016,512]{1,0:T(8,128)(2,1)}, u32[]{:S(2)}, u32[]{:S(2)}) collective-permute-start(bf16[4016,512]{1,0:T(8,128)(2,1)} %get-tuple-element.690), channel_id=1, source_target_pairs={{0,1},{1,2},{2,3},{3,4},{4,5},{5,6},{6,7},{7,0}} | collective-permute-start | bytes 12337160 | tf_op jit(solution)/shard_map/while/body/eval_jaxpr/ppermute | solution.py:53
  653.4 156.2 %collective-permute-start.2 = (f32[4016,512]{1,0:T(8,128)}, f32[4016,512]{1,0:T(8,128)}, u32[]{:S(2)}, u32[]{:S(2)}) collective-permute-start(f32[4016,512]{1,0:T(8,128)} %get-tuple-element.691), channel_id=1, source_target_pairs={{0,1},{1,2},{2,3},{3,4},{4,5},{5,6},{6,7},{7,0}} | collective-permute-start | bytes 24674312 | tf_op jit(solution)/shard_map/while/body/eval_jaxpr/ppermute | solution.py:54
  653.4 136.1 %collective-permute-start.1 = (bf16[4016,512]{1,0:T(8,128)(2,1)}, bf16[4016,512]{1,0:T(8,128)(2,1)}, u32[]{:S(2)}, u32[]{:S(2)}) collective-permute-start(bf16[4016,512]{1,0:T(8,128)(2,1)} %get-tuple-element.690), channel_id=1, source_target_pairs={{0,1},{1,2},{2,3},{3,4},{4,5},{5,6},{6,7},{7,0}} | collective-permute-start | bytes 12337160 | tf_op jit(solution)/shard_map/while/body/eval_jaxpr/ppermute | solution.py:53
  818.4 156.2 %collective-permute-start.2 = (f32[4016,512]{1,0:T(8,128)}, f32[4016,512]{1,0:T(8,128)}, u32[]{:S(2)}, u32[]{:S(2)}) collective-permute-start(f32[4016,512]{1,0:T(8,128)} %get-tuple-element.691), channel_id=1, source_target_pairs={{0,1},{1,2},{2,3},{3,4},{4,5},{5,6},{6,7},{7,0}} | collective-permute-start | bytes 24674312 | tf_op jit(solution)/shard_map/while/body/eval_jaxpr/ppermute | solution.py:54
  818.4 136.1 %collective-permute-start.1 = (bf16[4016,512]{1,0:T(8,128)(2,1)}, bf16[4016,512]{1,0:T(8,128)(2,1)}, u32[]{:S(2)}, u32[]{:S(2)}) collective-permute-start(bf16[4016,512]{1,0:T(8,128)(2,1)} %get-tuple-element.690), channel_id=1, source_target_pairs={{0,1},{1,2},{2,3},{3,4},{4,5},{5,6},{6,7},{7,0}} | collective-permute-start | bytes 12337160 | tf_op jit(solution)/shard_map/while/body/eval_jaxpr/ppermute | solution.py:53
  983.4 156.2 %collective-permute-start.2 = (f32[4016,512]{1,0:T(8,128)}, f32[4016,512]{1,0:T(8,128)}, u32[]{:S(2)}, u32[]{:S(2)}) collective-permute-start(f32[4016,512]{1,0:T(8,128)} %get-tuple-element.691), channel_id=1, source_target_pairs={{0,1},{1,2},{2,3},{3,4},{4,5},{5,6},{6,7},{7,0}} | collective-permute-start | bytes 24674312 | tf_op jit(solution)/shard_map/while/body/eval_jaxpr/ppermute | solution.py:54
  983.4 136.1 %collective-permute-start.1 = (bf16[4016,512]{1,0:T(8,128)(2,1)}, bf16[4016,512]{1,0:T(8,128)(2,1)}, u32[]{:S(2)}, u32[]{:S(2)}) collective-permute-start(bf16[4016,512]{1,0:T(8,128)(2,1)} %get-tuple-element.690), channel_id=1, source_target_pairs={{0,1},{1,2},{2,3},{3,4},{4,5},{5,6},{6,7},{7,0}} | collective-permute-start | bytes 12337160 | tf_op jit(solution)/shard_map/while/body/eval_jaxpr/ppermute | solution.py:53
  1148.4 156.2 %collective-permute-start.2 = (f32[4016,512]{1,0:T(8,128)}, f32[4016,512]{1,0:T(8,128)}, u32[]{:S(2)}, u32[]{:S(2)}) collective-permute-start(f32[4016,512]{1,0:T(8,128)} %get-tuple-element.691), channel_id=1, source_target_pairs={{0,1},{1,2},{2,3},{3,4},{4,5},{5,6},{6,7},{7,0}} | collective-permute-start | bytes 24674312 | tf_op jit(solution)/shard_map/while/body/eval_jaxpr/ppermute | solution.py:54
  1148.4 136.1 %collective-permute-start.1 = (bf16[4016,512]{1,0:T(8,128)(2,1)}, bf16[4016,512]{1,0:T(8,128)(2,1)}, u32[]{:S(2)}, u32[]{:S(2)}) collective-permute-start(bf16[4016,512]{1,0:T(8,128)(2,1)} %get-tuple-element.690), channel_id=1, source_target_pairs={{0,1},{1,2},{2,3},{3,4},{4,5},{5,6},{6,7},{7,0}} | collective-permute-start | bytes 12337160 | tf_op jit(solution)/shard_map/while/body/eval_jaxpr/ppermute | solution.py:53
  1313.4 156.2 %collective-permute-start.2 = (f32[4016,512]{1,0:T(8,128)}, f32[4016,512]{1,0:T(8,128)}, u32[]{:S(2)}, u32[]{:S(2)}) collective-permute-start(f32[4016,512]{1,0:T(8,128)} %get-tuple-element.691), channel_id=1, source_target_pairs={{0,1},{1,2},{2,3},{3,4},{4,5},{5,6},{6,7},{7,0}} | collective-permute-start | bytes 24674312 | tf_op jit(solution)/shard_map/while/body/eval_jaxpr/ppermute | solution.py:54
  1313.4 136.1 %collective-permute-start.1 = (bf16[4016,512]{1,0:T(8,128)(2,1)}, bf16[4016,512]{1,0:T(8,128)(2,1)}, u32[]{:S(2)}, u32[]{:S(2)}) collective-permute-start(bf16[4016,512]{1,0:T(8,128)(2,1)} %get-tuple-element.690), channel_id=1, source_target_pairs={{0,1},{1,2},{2,3},{3,4},{4,5},{5,6},{6,7},{7,0}} | collective-permute-start | bytes 12337160 | tf_op jit(solution)/shard_map/while/body/eval_jaxpr/ppermute | solution.py:53
  1478.4 156.2 %collective-permute-start.2 = (f32[4016,512]{1,0:T(8,128)}, f32[4016,512]{1,0:T(8,128)}, u32[]{:S(2)}, u32[]{:S(2)}) collective-permute-start(f32[4016,512]{1,0:T(8,128)} %get-tuple-element.691), channel_id=1, source_target_pairs={{0,1},{1,2},{2,3},{3,4},{4,5},{5,6},{6,7},{7,0}} | collective-permute-start | bytes 24674312 | tf_op jit(solution)/shard_map/while/body/eval_jaxpr/ppermute | solution.py:54
  1478.4 136.1 %collective-permute-start.1 = (bf16[4016,512]{1,0:T(8,128)(2,1)}, bf16[4016,512]{1,0:T(8,128)(2,1)}, u32[]{:S(2)}, u32[]{:S(2)}) collective-permute-start(bf16[4016,512]{1,0:T(8,128)(2,1)} %get-tuple-element.690), channel_id=1, source_target_pairs={{0,1},{1,2},{2,3},{3,4},{4,5},{5,6},{6,7},{7,0}} | collective-permute-start | bytes 12337160 | tf_op jit(solution)/shard_map/while/body/eval_jaxpr/ppermute | solution.py:53
  1643.4 116.0 %copy-start.4 = (f32[1024,512]{1,0:T(8,128)}, f32[1024,512]{1,0:T(8,128)S(1)}, u32[]{:S(2)}) copy-start(f32[1024,512]{1,0:T(8,128)S(1)} %get-tuple-element.719) | copy-start | bytes 6291460
  1643.4 108.4 %collective-permute-start.3 = (f32[4016,512]{1,0:T(8,128)}, f32[4016,512]{1,0:T(8,128)}, u32[]{:S(2)}, u32[]{:S(2)}) collective-permute-start(f32[4016,512]{1,0:T(8,128)} %get-tuple-element.452), channel_id=1, source_target_pairs={{0,1},{1,2},{2,3},{3,4},{4,5},{5,6},{6,7},{7,0}} | collective-permute-start | bytes 24674312 | tf_op jit(solution)/shard_map/ppermute | solution.py:60
where the time goes:
time: 1760 us
  waiting for transfers between devices  1290 us (73%)
  matrix products  241 us (14%)
  blocking collectives  108 us (6%)
  local copies, waits for them, and re-layouts  80.1 us (5%)
  other arithmetic  39.2 us (2%)
    ppermute x7, waiting for transfers between devices, bwd_body(): w_cur = lax.ppermute(w_cur, 'fsdp', ring_pairs)  952 us
    ppermute x7, waiting for transfers between devices, fwd_body(): w_cur = lax.ppermute(w_cur, 'fsdp', ring_pairs)  336 us
    dot_general x15, matrix products, block_logits(): lax.dot_general(hidden, w_blk, (((1,), (1,)), ((), ())), preferred_elemen...  117 us
    psum x1, blocking collectives, local_head(): lax.psum(jnp.sum(log_norm - tgt_logit) / tokens, 'fsdp').reshape(1)  108 us
    dot_general x8, matrix products, bwd_update(): lax.dot_general(dlogits, hidden, (((0,), (0,)), ((), ())), preferred_elem...  69 us
    while x21, local copies, waits for them, and re-layouts  61.4 us
    dot_general x8, matrix products, bwd_update(): dh_part = jnp.dot(dlogits, w_blk, preferred_element_type=jnp.float32)  55.1 us
    reduce_sum x8, other arithmetic, fwd_update(): tgt_logit = tgt_logit + jnp.sum(jnp.where(is_target, logits, 0.0), axis=1)  38.4 us
  transfers between devices with their start and end apart: 22, of which 14 were waited for; matrix products, arithmetic and copies ran while one was open for 8% of the time, Pallas kernels for 0%

commit v1 on v0

v1 whole, which is shorter than its diff:
```python
import jax
import jax.numpy as jnp
from jax import lax
from jax.sharding import PartitionSpec as P


def solution(mesh):
    groups = mesh.shape["fsdp"]
    tok_spec = P(("dp", "fsdp"), None)

    def local_head(hidden, targets, weight):
        tok_loc = hidden.shape[0]
        shard_rows = weight.shape[0]
        tokens = tok_loc * groups
        rank_id = lax.axis_index("fsdp")
        hid = lax.all_gather(hidden, "fsdp", tiled=True)
        tgt = lax.all_gather(targets, "fsdp", tiled=True)
        row_ids = jnp.arange(shard_rows, dtype=jnp.int32)
        is_target = row_ids[:, None] == (tgt - rank_id * shard_rows)[None, :]
        logits = lax.dot_general(weight, hid, (((1,), (1,)), ((), ())), preferred_element_type=jnp.float32)
        loc_max = jnp.max(logits, axis=0)
        glob_max = lax.pmax(loc_max, "fsdp")
        exps = jnp.exp(logits - glob_max[None, :])
        loc_sum = jnp.sum(exps, axis=0)
        loc_tgt = jnp.sum(jnp.where(is_target, logits, 0.0), axis=0)
        glob_sum, glob_tgt = lax.psum((loc_sum, loc_tgt), "fsdp")
        log_norm = glob_max + jnp.log(glob_sum)
        loss_val = (jnp.sum(log_norm - glob_tgt) / tokens).reshape(1)
        dz = ((jnp.exp(logits - log_norm[None, :]) - is_target.astype(jnp.float32)) / tokens).astype(jnp.bfloat16)
        dw = jnp.dot(dz, hid, preferred_element_type=jnp.float32)
        dh = lax.dot_general(dz, weight, (((0,), (0,)), ((), ())), preferred_element_type=jnp.float32)
        dh = lax.psum_scatter(dh, "fsdp", scatter_dimension=0, tiled=True)
        return loss_val, dh, dw

    return jax.shard_map(local_head, mesh=mesh, in_specs=(tok_spec, P(("dp", "fsdp")), P("fsdp", None)), out_specs=(P("dp"), tok_spec, tok_spec), check_vma=False)
```

time: 1760 us -> 391 us (0.22)
  waiting for transfers between devices: 1290 us -> 137 us
  matrix products: 241 us -> 159 us
  local copies, waits for them, and re-layouts: 80.1 us -> 0 us
  blocking collectives: 108 us -> 36.4 us
    ppermute x22 -> x0, waiting for transfers between devices: 1290 us -> none  [the longest x7 952 us: bwd_body(): w_cur = lax.ppermute(w_cur, 'fsdp', ring_pairs)]
    psum x1 -> x0, blocking collectives: 108 us -> none  [local_head(): lax.psum(jnp.sum(log_norm - tgt_logit) / tokens, 'fsdp').reshape(1)]
    dot_general x31 -> x3, matrix products: 241 us -> 159 us  [the longest x1 53.2 us: local_head(): lax.dot_general(dz, weight, (((0,), (0,)), ((), ())), preferred_element_t...]
    while x21 -> x0, local copies, waits for them, and re-layouts: 61.4 us -> none
    reduce_scatter x0 -> x1, waiting for transfers between devices: none -> 53.2 us  [local_head(): dh = lax.psum_scatter(dh, 'fsdp', scatter_dimension=0, tiled=True)]
    psum x0 -> x1, waiting for transfers between devices: none -> 43.9 us  [local_head(): glob_sum, glob_tgt = lax.psum((loc_sum, loc_tgt), 'fsdp')]
    all_gather x0 -> x1, waiting for transfers between devices: none -> 39.1 us  [local_head(): hid = lax.all_gather(hidden, 'fsdp', tiled=True)]
    pmax x0 -> x1, blocking collectives: none -> 22.3 us  [local_head(): glob_max = lax.pmax(loc_max, 'fsdp')]
  transfers between devices with their start and end apart: 22 -> 3, of which waited for: 14 -> 3; matrix products, arithmetic and copies ran while one was open for 8% -> 13% of each run, Pallas kernels for 0% -> 0%
where the time goes in v1:
time: 391 us; the launch traced here: 390 us
  matrix products  159 us (41%)
  waiting for transfers between devices  137 us (35%)
  other arithmetic  42.5 us (11%)
  blocking collectives  36.4 us (9%)
  between operations  15.5 us (4%)
    reduce_scatter x1, waiting for transfers between devices, local_head(): dh = lax.psum_scatter(dh, 'fsdp', scatter_dimension=0, tiled=True)  53.2 us
    dot_general x1, matrix products, local_head(): lax.dot_general(dz, weight, (((0,), (0,)), ((), ())), preferred_element_t...  53.2 us
    dot_general x1, matrix products, local_head(): lax.dot_general(weight, hid, (((1,), (1,)), ((), ())), preferred_element_...  52.8 us
    dot_general x1, matrix products, local_head(): dw = jnp.dot(dz, hid, preferred_element_type=jnp.float32)  52.6 us
    psum x1, waiting for transfers between devices, local_head(): glob_sum, glob_tgt = lax.psum((loc_sum, loc_tgt), 'fsdp')  43.9 us
    reduce_sum x1, other arithmetic, local_head(): loc_tgt = jnp.sum(jnp.where(is_target, logits, 0.0), axis=0)  41.1 us
    all_gather x1, waiting for transfers between devices, local_head(): hid = lax.all_gather(hidden, 'fsdp', tiled=True)  39.1 us
    pmax x1, blocking collectives, local_head(): glob_max = lax.pmax(loc_max, 'fsdp')  22.3 us
  transfers between devices with their start and end apart: 3, of which 3 were waited for; matrix products, arithmetic and copies ran while one was open for 13% of the time, Pallas kernels for 0%

profile of v1, /device:TPU:0, one launch (start us, length us, event | category | flops | bytes accessed | tf_op | source)
XLA Modules:
  0.0 390.1 jit_solution(15510201902372649120)
XLA Ops:
  7.2 0.0 all-gather.2.cloned.1.call-start
  7.2 0.7 all-gather.2.cloned.1.call-update
  7.9 0.0 all-reduce.3.cloned.1.call-start
  7.9 14.0 %all_gather.7 = s32[8192]{0:T(1024)S(1)} all-gather(s32[1024]{0:T(1024)} %param.4), channel_id=1, replica_groups=mesh['dp'=1,'fsdp'=8] {'fsdp'}, dimensions={0}, use_global_device_ids=true | all-gather | bytes 36864 | tf_op jit(solution)/shard_map/all_gather | solution.py:17
  22.0 39.1 %all-gather.2.cloned.1.call-done = bf16[8192,512]{1,0:T(8,128)(2,1)} async-done(((bf16[1024,512]{1,0:T(8,128)(2,1)}), bf16[8192,512]{1,0:T(8,128)(2,1)}) %all-gather.2.cloned.1.call-update) | async-done | bytes 8388624 | tf_op jit(solution)/shard_map/all_gather | solution.py:16
  61.1 52.8 %fusion.2 = (f32[8192]{0:T(1024)S(1)}, f32[4016,8192]{1,0:T(8,128)}) fusion(bf16[4016,512]{1,0:T(8,128)(2,1)} %param.5, bf16[8192,512]{1,0:T(8,128)(2,1)} %all-gather.2.cloned.1.call-done), kind=kOutput, calls=%fused_computation.9 | convolution fusion | flops 33721540608 | bytes 144130048 | tf_op jit(solution)/shard_map/dot_general | solution.py:20
  113.9 22.3 %pmax.7 = f32[8192]{0:T(1024)S(1)} all-reduce(f32[8192]{0:T(1024)S(1)} %get-tuple-element.9), channel_id=1, replica_groups=mesh['dp'=1,'fsdp'=8] {'fsdp'}, use_global_device_ids=true, to_apply=%region_1.0 | all-reduce | flops 8192 | bytes 65536 | tf_op jit(solution)/shard_map/pmax | solution.py:22
  136.2 41.1 %select_reduce_fusion = (f32[8192]{0:T(1024)}, f32[8192]{0:T(1024)}) fusion(f32[4016,8192]{1,0:T(8,128)} %get-tuple-element.10, s32[8192]{0:T(1024)S(1)} %broadcast_subtract_fusion, f32[8192]{0:T(1024)S(1)} %pmax.7), kind=kLoop, calls=%fused_computation.1 | loop fusion | flops 164478976 | bytes 131727360 | tf_op jit(solution)/shard_map/reduce_sum | solution.py:25
  177.3 0.0 all-reduce.3.cloned.1.call-update
  177.3 0.2 reduce-scatter.2.cloned.1.call-start
  177.5 43.9 %all-reduce.3.cloned.1.call-done = (f32[8192]{0:T(1024)}, f32[8192]{0:T(1024)}) async-done(((f32[8192]{0:T(1024)}, f32[8192]{0:T(1024)}), (f32[8192]{0:T(1024)}, f32[8192]{0:T(1024)})) %all-reduce.3.cloned.1.call-update) | async-done | bytes 65552 | tf_op jit(solution)/shard_map/psum | solution.py:26
  221.4 1.4 subtract_reduce_fusion
  222.8 53.2 %fusion.1 = f32[8192,512]{1,0:T(8,128)} fusion(bf16[4016,512]{1,0:T(8,128)(2,1)} %param.5, f32[4016,8192]{1,0:T(8,128)} %get-tuple-element.10, f32[8192]{0:T(1024)S(1)} %get-tuple-element.8, s32[8192]{0:T(1024)S(1)} %broadcast_subtract_fusion), kind=kOutput, calls=%fused_computation.8 | convolution fusion | flops 33886044160 | bytes 152551424 | tf_op jit(solution)/shard_map/dot_general | solution.py:31
  276.0 0.0 reduce-scatter.2.cloned.1.call-update
  276.7 52.6 %fusion = f32[4016,512]{1,0:T(8,128)} fusion(bf16[8192,512]{1,0:T(8,128)(2,1)} %all-gather.2.cloned.1.call-done, f32[4016,8192]{1,0:T(8,128)} %get-tuple-element.10, f32[8192]{0:T(1024)S(1)} %get-tuple-element.8, s32[8192]{0:T(1024)S(1)} %broadcast_subtract_fusion), kind=kOutput, calls=%fused_computation.7 | convolution fusion | flops 33886044160 | bytes 148275200 | tf_op jit(solution)/shard_map/dot_general | solution.py:30
  329.3 53.2 %reduce-scatter.2.cloned.1.call-done = f32[1024,512]{1,0:T(8,128)} async-done(((f32[8192,512]{1,0:T(8,128)}), f32[1024,512]{1,0:T(8,128)}) %reduce-scatter.2.cloned.1.call-update) | async-done | bytes 2097168 | tf_op jit(solution)/shard_map/reduce_scatter | solution.py:32
  (1 shorter events, 0.0 us)
Async XLA Ops:
  7.2 53.9 %all-gather.2.cloned.1.call-start = ((), (), s32[]{:S(2)}) async-start(), calls=%async_computation.1 | async-start | bytes 9437184 | tf_op jit(solution)/shard_map/all_gather | solution.py:16
  7.9 213.5 %all-reduce.3.cloned.1.call-start = ((), (), s32[]{:S(2)}) async-start(), calls=%async_computation.3 | async-start | bytes 131072 | tf_op jit(solution)/shard_map/psum | solution.py:26
  177.3 205.2 %reduce-scatter.2.cloned.1.call-start = ((), (), s32[]{:S(2)}) async-start(), calls=%async_computation.2 | async-start | bytes 18874368 | tf_op jit(solution)/shard_map/reduce_scatter | solution.py:32
Sparse Core Ops, SparseCore 0:
  9.8 51.2 all-gather.1
  177.4 43.9 all-reduce.2
  276.1 106.2 reduce-scatter.1

commit v2 on v1

v2 whole, which is shorter than its diff:
```python
import functools

import jax
import jax.numpy as jnp
from jax import lax
from jax.experimental import pallas as pl
from jax.experimental.pallas import tpu as pltpu
from jax.sharding import PartitionSpec as P

PIECE = 128
CHIPS = 4
STEP_TOK = PIECE * CHIPS
CHUNK = 512
F32 = jnp.float32


def head_kernel(hid, tgt, w, loss_out, dh_out, dw_out, wt, probs, dw_acc, hbuf, tbuf, zbuf_a, zbuf_b, dz_a, dz_b, dh_acc,
                runmax, factor, tgt_sum, lse_sum, st_send, st_recv, tt_send, tt_recv, pair_buf, s1_buf, r1_buf, s2_buf, r2_buf,
                own_buf, out_stage, h_sem, h_send, fw_send, t_sem, t_send, st_rsem, st_ssem, tt_sem, pair_sem, s1_sem, s2_sem,
                out_sem, out_send, dw_sem):
    tok_loc, width = hid.shape
    vocab = w.shape[0]
    steps = 2 * tok_loc // PIECE
    tokens = tok_loc * 2 * CHIPS
    half = width // 2
    n_chunks = -(-vocab // CHUNK)
    last_rows = vocab - (n_chunks - 1) * CHUNK
    inv_tokens = 1.0 / tokens
    zbufs, dzs = (zbuf_a, zbuf_b), (dz_a, dz_b)

    me = lax.axis_index("fsdp")
    core, chip = me % 2, me // 2
    x, y = chip % 2, chip // 2
    partner = chip * 2 + 1 - core
    chip_x, chip_y, chip_d = y * 2 + (1 - x), (1 - y) * 2 + x, (1 - y) * 2 + (1 - x)
    chip_1 = (1 - core) * chip_x + core * chip_y
    chip_2 = (1 - core) * chip_y + core * chip_x

    def remote(src, dst, send, recv, dev):
        return pltpu.make_async_remote_copy(src_ref=src, dst_ref=dst, send_sem=send, recv_sem=recv, device_id={"fsdp": dev},
                                            device_id_type=pl.DeviceIdType.MESH)

    def wait_bytes(ref, sem):
        pltpu.make_async_copy(ref, ref, sem).wait()

    def chunk_rows(c):
        return CHUNK if c < n_chunks - 1 else last_rows

    def h_sends(q):
        s = 2 * q + core
        rows = pl.ds(pl.multiple_of(q * PIECE, PIECE), PIECE)
        cols = pl.ds(pl.multiple_of(chip * PIECE, PIECE), PIECE)
        return [remote(hid.at[rows], hbuf.at[s, cols], h_send.at[i, q], h_sem.at[s], peer * 2 + core)
                for i, peer in enumerate((chip_x, chip_y, chip_d))]

    def h_forward(s):
        return remote(hbuf.at[s], hbuf.at[s], fw_send.at[s // 2], h_sem.at[s], partner)

    def stats_sends(s):
        return [remote(st_send.at[s], st_recv.at[s, me], st_ssem.at[s], st_rsem.at[s], (me + i) % (2 * CHIPS)) for i in range(1, 2 * CHIPS)]

    def pair_copy(s):
        rows = pl.ds(pl.multiple_of((1 - core) * half, half), half)
        return remote(dh_acc.at[s % 2, rows], pair_buf.at[s % 2], pair_sem.at[0, s % 2], pair_sem.at[1, s % 2], partner)

    def s1_copies(s):
        sl = s % 2
        return [remote(s1_buf.at[sl, block], r1_buf.at[sl, i], s1_sem.at[0, sl], s1_sem.at[1, sl], chip_1 * 2 + core)
                for i, block in enumerate((chip_1, chip_d))]

    def s2_copy(s):
        return remote(s2_buf.at[s % 2], r2_buf.at[s % 2], s2_sem.at[0, s % 2], s2_sem.at[1, s % 2], chip_2 * 2 + core)

    def out_dst(s):
        return dh_out.at[pl.ds(pl.multiple_of(s // 2 * PIECE, PIECE), PIECE), pl.ds(pl.multiple_of(core * half, half), half)]

    def out_remote(s):
        return remote(out_stage.at[s], out_dst(s), out_send.at[s // 2], out_sem, partner)

    def reduce_stages(u):
        @pl.when((u >= 6) & (u < steps + 6))
        def _():
            s = u - 6
            wait_bytes(r2_buf.at[s % 2], s2_sem.at[1, s % 2])
            out_stage[s] = (own_buf[s % 2] + r2_buf[s % 2]).T

            @pl.when(s % 2 == core)
            def _():
                pltpu.make_async_copy(out_stage.at[s], out_dst(s), out_sem).start()

            @pl.when(s % 2 != core)
            def _():
                out_remote(s).start()

        @pl.when((u >= 5) & (u < steps + 5))
        def _():
            s = u - 5
            sl = s % 2
            wait_bytes(r1_buf.at[sl], s1_sem.at[1, sl])

            @pl.when(s >= 2)
            def _():
                wait_bytes(s2_buf.at[sl], s2_sem.at[0, sl])

            s2_buf[sl] = s1_buf[sl, chip_2] + r1_buf[sl, 1]
            own_buf[sl] = s1_buf[sl, chip] + r1_buf[sl, 0]
            s2_copy(s).start()

        @pl.when((u >= 4) & (u < steps + 4))
        def _():
            s = u - 4
            sl = s % 2
            wait_bytes(pair_buf.at[sl], pair_sem.at[1, sl])
            wait_bytes(pair_buf.at[sl], pair_sem.at[0, sl])

            @pl.when(s >= 2)
            def _():
                wait_bytes(r1_buf.at[sl], s1_sem.at[0, sl])

            rows = pl.ds(pl.multiple_of(core * half, half), half)
            for j in range(CHIPS):
                cols = pl.ds(j * PIECE, PIECE)
                s1_buf[sl, j] = dh_acc[sl, rows, cols] + pair_buf[sl, :, cols]
            for copy in s1_copies(s):
                copy.start()

        @pl.when((u >= 3) & (u < steps + 3))
        def _():
            pair_copy(u - 3).start()

    def h_stages(u):
        @pl.when((u + 4 < steps) & (u % 2 == core))
        def _():
            for copy in h_sends((u + 4) // 2):
                copy.start()

        @pl.when((u + 1 < steps) & ((u + 1) % 2 == core))
        def _():
            wait_bytes(hbuf.at[u + 1], h_sem.at[u + 1])
            h_forward(u + 1).start()

        @pl.when((u < steps) & (u % 2 != core))
        def _():
            wait_bytes(hbuf.at[u], h_sem.at[u])

    def target_row(s):
        row = jnp.concatenate([tbuf[2 * j + s % 2, pl.ds(s // 2, 1), :] for j in range(CHIPS)], axis=1)
        return row - me * vocab

    def finish_stats(s):
        wait_bytes(st_recv.at[s], st_rsem.at[s])
        stats = st_recv[s]
        m, e = stats[:, :CHIPS], stats[:, CHIPS:]
        top = jnp.max(m, axis=0)
        lse = top + jnp.log(jnp.sum(e * jnp.exp(m - top[None]), axis=0))
        lse_sum[...] += lse
        lse_row = jnp.concatenate([lse[j:j + 1] for j in range(CHIPS)], axis=1)
        factor[...] = jnp.exp(runmax[s % 2] - lse_row) * inv_tokens

    def chunks(u, fwd, bwd):
        par = u % 2
        if fwd:
            h_f = hbuf.at[u]
            t_f = target_row(u)
        if bwd:
            s = u - 2
            h_b = hbuf.at[s]
            t_b = target_row(s)
        run_m = run_s = tacc = None
        for c in range(n_chunks + 1):
            if c < n_chunks:
                lo, n = c * CHUNK, chunk_rows(c)
                if bwd:
                    dz_ref = dzs[c % 2]
                    ids = lax.broadcasted_iota(jnp.int32, (n, STEP_TOK), 0) + lo
                    hot = jnp.where(ids == t_b, inv_tokens, 0.0)
                    dz_ref[:n] = (probs[par, lo:lo + n] * factor[c:c + 1] - hot).astype(jnp.bfloat16)
                    if n < CHUNK:
                        dz_ref[n:] = jnp.zeros((CHUNK - n, STEP_TOK), jnp.bfloat16)
                if fwd:
                    zbufs[c % 2][:n] = lax.dot_general(w[lo:lo + n], h_f[...], (((1,), (1,)), ((), ())), preferred_element_type=F32)
            if c > 0:
                p = c - 1
                lo, n = p * CHUNK, chunk_rows(p)
                if bwd:
                    dz_ref = dzs[p % 2]
                    part = jnp.dot(wt[:, lo:lo + CHUNK], dz_ref[...], preferred_element_type=F32)
                    if p == 0:
                        dh_acc[par] = part
                    else:
                        dh_acc[par] += part
                    dw_acc[lo:lo + n] += jnp.dot(dz_ref[:n], h_b[...], preferred_element_type=F32)
                if fwd:
                    z = zbufs[p % 2][:n]
                    new_m = jnp.max(z, axis=0, keepdims=True)
                    if p > 0:
                        new_m = jnp.maximum(new_m, run_m)
                    e = jnp.exp(z - new_m)
                    probs[par, lo:lo + n] = e
                    part = jnp.sum(e, axis=0, keepdims=True)
                    ids = lax.broadcasted_iota(jnp.int32, (n, STEP_TOK), 0) + lo
                    hit = jnp.sum(jnp.where(ids == t_f, z, 0.0), axis=0, keepdims=True)
                    if p > 0:
                        part = run_s * jnp.exp(run_m - new_m) + part
                        hit = tacc + hit
                    run_m, run_s, tacc = new_m, part, hit
                    runmax[par, p:p + 1] = new_m
        if fwd:
            for j in range(CHIPS):
                cols = slice(j * PIECE, (j + 1) * PIECE)
                st_send[u, j:j + 1] = run_m[:, cols]
                st_send[u, CHIPS + j:CHIPS + j + 1] = run_s[:, cols]
            tgt_sum[...] += tacc
            pltpu.make_async_copy(st_send.at[u], st_recv.at[u, me], st_rsem.at[u]).start()
            for copy in stats_sends(u):
                copy.start()

    def prepare(u):
        reduce_stages(u)
        h_stages(u)

    barrier = pltpu.get_barrier_semaphore()
    for i in range(1, 2 * CHIPS):
        pl.semaphore_signal(barrier, inc=1, device_id={"fsdp": (me + i) % (2 * CHIPS)}, device_id_type=pl.DeviceIdType.MESH)
    pl.semaphore_wait(barrier, 2 * CHIPS - 1)

    def own_piece(q, _):
        s = 2 * q + core
        pltpu.make_async_copy(hid.at[pl.ds(pl.multiple_of(q * PIECE, PIECE), PIECE)],
                              hbuf.at[s, pl.ds(pl.multiple_of(chip * PIECE, PIECE), PIECE)], h_sem.at[s]).start()
        return 0

    lax.fori_loop(0, steps // 2, own_piece, 0)
    for copy in h_sends(0):
        copy.start()
    pltpu.make_async_copy(tgt, tbuf.at[me], t_sem).start()
    t_copies = [remote(tgt, tbuf.at[me], t_send, t_sem, (me + i) % (2 * CHIPS)) for i in range(1, 2 * CHIPS)]
    for copy in t_copies:
        copy.start()
    for copy in h_sends(1):
        copy.start()

    for c in range(n_chunks):
        n = chunk_rows(c)
        wt[:, c * CHUNK:c * CHUNK + n] = w[c * CHUNK:c * CHUNK + n].T
    if last_rows < CHUNK:
        wt[:, vocab:] = jnp.zeros((width, n_chunks * CHUNK - vocab), jnp.bfloat16)
    dw_acc[...] = jnp.zeros_like(dw_acc)
    tgt_sum[...] = jnp.zeros_like(tgt_sum)
    lse_sum[...] = jnp.zeros_like(lse_sum)

    @pl.when(core == 0)
    def _():
        wait_bytes(hbuf.at[0], h_sem.at[0])
        h_forward(0).start()

    wait_bytes(tbuf, t_sem)

    def fwd_step(u, _):
        prepare(u)
        chunks(u, True, False)
        return 0

    def both_step(u, _):
        prepare(u)
        finish_stats(u - 2)
        chunks(u, True, True)
        return 0

    def bwd_step(u, _):
        prepare(u)
        finish_stats(u - 2)
        chunks(u, False, True)
        return 0

    def tail_step(u, _):
        reduce_stages(u)
        return 0

    lax.fori_loop(0, 2, fwd_step, 0)
    lax.fori_loop(2, steps, both_step, 0)
    row = tgt_sum[...]
    tile = jnp.concatenate([row[:, j * PIECE:(j + 1) * PIECE] for j in range(CHIPS)] + [jnp.zeros((8 - CHIPS, PIECE), F32)], axis=0)
    tt_send[...] = tile
    pltpu.make_async_copy(tt_send, tt_recv.at[me], tt_sem.at[1]).start()
    for i in range(1, 2 * CHIPS):
        remote(tt_send, tt_recv.at[me], tt_sem.at[0], tt_sem.at[1], (me + i) % (2 * CHIPS)).start()
    lax.fori_loop(steps, steps + 2, bwd_step, 0)
    dw_copy = pltpu.make_async_copy(dw_acc, dw_out, dw_sem)
    dw_copy.start()
    wait_bytes(tt_recv, tt_sem.at[1])
    loss_out[0] = (jnp.sum(lse_sum[...]) - jnp.sum(tt_recv[...])) * inv_tokens
    lax.fori_loop(steps + 2, steps + 6, tail_step, 0)

    wait_bytes(dh_out, out_sem)
    dw_copy.wait()
    peers = 2 * CHIPS - 1
    wait_bytes(tbuf.at[:peers], t_send)
    wait_bytes(tt_recv.at[:peers], tt_sem.at[0])

    def drain_pieces(q, _):
        for copy in h_sends(q):
            copy.wait_send()
        wait_bytes(hbuf.at[2 * q + core], fw_send.at[q])
        wait_bytes(out_stage.at[2 * q], out_send.at[q])
        return 0

    def drain_stats(s, _):
        wait_bytes(st_recv.at[s, :peers], st_ssem.at[s])
        return 0

    lax.fori_loop(0, steps // 2, drain_pieces, 0)
    lax.fori_loop(0, steps, drain_stats, 0)
    for sl in range(2):
        wait_bytes(r1_buf.at[sl], s1_sem.at[0, sl])
        wait_bytes(s2_buf.at[sl], s2_sem.at[0, sl])


def solution(mesh):
    groups = mesh.shape["fsdp"]
    tok_spec = P(("dp", "fsdp"), None)

    def local_head(hidden, targets, weight):
        tok_loc, width = hidden.shape
        vocab = weight.shape[0]
        steps = 2 * tok_loc // PIECE
        padded = -(-vocab // CHUNK) * CHUNK
        half = width // 2
        dma, bf16 = pltpu.SemaphoreType.DMA, jnp.bfloat16
        vmem = pl.BlockSpec(memory_space=pltpu.VMEM)
        anyspace = pl.BlockSpec(memory_space=pl.ANY)
        scratch = [
            pltpu.VMEM((width, padded), bf16),
            pltpu.VMEM((2, padded, STEP_TOK), F32),
            pltpu.VMEM((vocab, width), F32),
            pltpu.VMEM((steps, STEP_TOK, width), bf16),
            pltpu.VMEM((groups, tok_loc // PIECE, PIECE), jnp.int32),
            pltpu.VMEM((CHUNK, STEP_TOK), F32), pltpu.VMEM((CHUNK, STEP_TOK), F32),
            pltpu.VMEM((CHUNK, STEP_TOK), bf16), pltpu.VMEM((CHUNK, STEP_TOK), bf16),
            pltpu.VMEM((2, width, STEP_TOK), F32),
            pltpu.VMEM((2, padded // CHUNK, STEP_TOK), F32),
            pltpu.VMEM((padded // CHUNK, STEP_TOK), F32),
            pltpu.VMEM((1, STEP_TOK), F32),
            pltpu.VMEM((CHIPS, PIECE), F32),
            pltpu.VMEM((steps, 8, PIECE), F32),
            pltpu.VMEM((steps, groups, 8, PIECE), F32),
            pltpu.VMEM((8, PIECE), F32),
            pltpu.VMEM((groups, 8, PIECE), F32),
            pltpu.VMEM((2, half, STEP_TOK), F32),
            pltpu.VMEM((2, CHIPS, half, PIECE), F32),
            pltpu.VMEM((2, 2, half, PIECE), F32),
            pltpu.VMEM((2, half, PIECE), F32),
            pltpu.VMEM((2, half, PIECE), F32),
            pltpu.VMEM((2, half, PIECE), F32),
            pltpu.VMEM((steps, PIECE, half), F32),
            dma((steps,)), dma((3, steps // 2)), dma((steps // 2,)),
            dma(()), dma(()),
            dma((steps,)), dma((steps,)),
            dma((2,)), dma((2, 2)), dma((2, 2)), dma((2, 2)),
            dma(()), dma((steps // 2,)), dma(()),
        ]
        flops = 6 * tok_loc * groups * vocab * width
        return pl.pallas_call(
            head_kernel,
            out_shape=(jax.ShapeDtypeStruct((1,), F32), jax.ShapeDtypeStruct((tok_loc, width), F32), jax.ShapeDtypeStruct((vocab, width), F32)),
            in_specs=[vmem, vmem, vmem],
            out_specs=(pl.BlockSpec(memory_space=pltpu.SMEM), anyspace, anyspace),
            scratch_shapes=scratch,
            compiler_params=pltpu.CompilerParams(collective_id=0, has_side_effects=True, vmem_limit_bytes=67_043_328),
            cost_estimate=pl.CostEstimate(flops=flops, bytes_accessed=20_000_000, transcendentals=tok_loc * groups * vocab),
        )(hidden, targets.reshape(tok_loc // PIECE, PIECE), weight)

    return jax.shard_map(local_head, mesh=mesh, in_specs=(tok_spec, P(("dp", "fsdp")), P("fsdp", None)), out_specs=(P("dp"), tok_spec, tok_spec), check_vma=False)
```

time: 391 us -> 187 us (0.48)
  Pallas kernels: 0 us -> 173 us
  matrix products: 159 us -> 0 us
  waiting for transfers between devices: 137 us -> 0 us
  other arithmetic: 42.5 us -> 0 us
  blocking collectives: 36.4 us -> 0 us
  between operations: 15.5 us -> 2.4 us
  local copies, waits for them, and re-layouts: 0 us -> 10.7 us
    pallas_call x0 -> x1, Pallas kernels: none -> 173 us  [local_head(): pl.pallas_call(head_kernel, out_shape=(jax.ShapeDtypeStruct((1,), F32), j...]
    dot_general x3 -> x0, matrix products: 159 us -> none  [the longest x1 53.2 us: local_head(): lax.dot_general(dz, weight, (((0,), (0,)), ((), ())), preferred_element_t...]
    reduce_scatter x1 -> x0, waiting for transfers between devices: 53.2 us -> none  [local_head(): dh = lax.psum_scatter(dh, 'fsdp', scatter_dimension=0, tiled=True)]
    psum x1 -> x0, waiting for transfers between devices: 43.9 us -> none  [local_head(): glob_sum, glob_tgt = lax.psum((loc_sum, loc_tgt), 'fsdp')]
    reduce_sum x2 -> x0, other arithmetic: 42.5 us -> none  [the longest x1 41.1 us: local_head(): loc_tgt = jnp.sum(jnp.where(is_target, logits, 0.0), axis=0)]
    all_gather x1 -> x0, waiting for transfers between devices: 39.1 us -> none  [local_head(): hid = lax.all_gather(hidden, 'fsdp', tiled=True)]
    pmax x1 -> x0, blocking collectives: 22.3 us -> none  [local_head(): glob_max = lax.pmax(loc_max, 'fsdp')]
    all_gather x1 -> x0, blocking collectives: 14 us -> none  [local_head(): tgt = lax.all_gather(targets, 'fsdp', tiled=True)]
  transfers between devices with their start and end apart: 3 -> 0, of which waited for: 3 -> 0; matrix products, arithmetic and copies ran while one was open for 13% -> 0% of each run, Pallas kernels for 0% -> 0%
where the time goes in v2:
time: 187 us; the launch traced here: 186 us
  Pallas kernels  173 us (93%)
  local copies, waits for them, and re-layouts  10.7 us (6%)
  between operations  2.4 us (1%)
    pallas_call x1, Pallas kernels, local_head(): pl.pallas_call(head_kernel, out_shape=(jax.ShapeDtypeStruct((1,), F32), j...  173 us
    unnamed x2, local copies, waits for them, and re-layouts  10.7 us

profile of v2, /device:TPU:0, one launch (start us, length us, event | category | flops | bytes accessed | tf_op | source)
XLA Modules:
  0.0 186.4 jit_solution(9799648715064815779)
XLA Ops:
  0.6 173.3 %shard_map.58 = (f32[1]{0:T(128)}, f32[1024,512]{1,0:T(8,128)}, f32[4016,512]{1,0:T(8,128)}) custom-call(bf16[1024,512]{1,0:T(8,128)(2,1)} %hid.1, s32[8,128]{1,0:T(8,128)} %bitcast.1, bf16[4016,512]{1,0:T(8,128)(2,1)} %w.1), custom_call_target="tpu_custom_call" | custom-call | flops 101065949184 | bytes 20000000 | tf_op jit(solution)/shard_map/pallas_call | solution.py:363
  174.6 3.1 %copy.10 = f32[1024,512]{1,0:T(8,128)} copy(f32[1024,512]{1,0:T(8,128)} %get-tuple-element.7) | data formatting | bytes 4194304
  177.7 7.6 %copy.11 = f32[4016,512]{1,0:T(8,128)} copy(f32[4016,512]{1,0:T(8,128)} %get-tuple-element.8) | data formatting | bytes 16449536

commit v3 on v2

--- a/solution.py
+++ b/solution.py
@@ -10,14 +10,15 @@
 PIECE = 128
 CHIPS = 4
 STEP_TOK = PIECE * CHIPS
+DIRECT = 4
 CHUNK = 512
 F32 = jnp.float32
 
 
-def head_kernel(hid, tgt, w, loss_out, dh_out, dw_out, wt, probs, dw_acc, hbuf, tbuf, zbuf_a, zbuf_b, dz_a, dz_b, dh_acc,
+def head_kernel(hid, tgt, w_in, loss_out, dh_out, dw_out, w, wt, probs, hbuf, tbuf, zbuf_a, zbuf_b, dz_a, dz_b, dh_acc,
                 runmax, factor, tgt_sum, lse_sum, st_send, st_recv, tt_send, tt_recv, pair_buf, s1_buf, r1_buf, s2_buf, r2_buf,
-                own_buf, out_stage, h_sem, h_send, fw_send, t_sem, t_send, st_rsem, st_ssem, tt_sem, pair_sem, s1_sem, s2_sem,
-                out_sem, out_send, dw_sem):
+                own_buf, out_stage, w_sem, h_own, h_recv, h_fwd, h_send, fw_send, t_sem, t_send, st_rsem, st_ssem, tt_sem, pair_sem,
+                s1_sem, s2_sem, out_sem, out_send):
     tok_loc, width = hid.shape
     vocab = w.shape[0]
     steps = 2 * tok_loc // PIECE
@@ -26,6 +27,7 @@
     n_chunks = -(-vocab // CHUNK)
     last_rows = vocab - (n_chunks - 1) * CHUNK
     inv_tokens = 1.0 / tokens
+    dw_acc = dw_out
     zbufs, dzs = (zbuf_a, zbuf_b), (dz_a, dz_b)
 
     me = lax.axis_index("fsdp")
@@ -46,15 +48,21 @@
     def chunk_rows(c):
         return CHUNK if c < n_chunks - 1 else last_rows
 
-    def h_sends(q):
+    def piece(s, of_chip, lo=0, n=PIECE):
+        return hbuf.at[s, pl.ds(pl.multiple_of(of_chip * PIECE + lo, n), n)]
+
+    def h_sends(q, direct):
         s = 2 * q + core
-        rows = pl.ds(pl.multiple_of(q * PIECE, PIECE), PIECE)
-        cols = pl.ds(pl.multiple_of(chip * PIECE, PIECE), PIECE)
-        return [remote(hid.at[rows], hbuf.at[s, cols], h_send.at[i, q], h_sem.at[s], peer * 2 + core)
-                for i, peer in enumerate((chip_x, chip_y, chip_d))]
+        peers = (chip_x, chip_y, chip_d)[:3 if direct else 2]
+        return [remote(piece(s, chip), piece(s, chip), h_send.at[i, q], h_recv.at[i, q], peer * 2 + core) for i, peer in enumerate(peers)]
+
+    def h_relays(s):
+        q = s // 2
+        return [remote(piece(s, src, lo, PIECE // 2), piece(s, src, lo, PIECE // 2), h_send.at[3 + i, q], h_recv.at[2, q], dst * 2 + core)
+                for i, (src, dst, lo) in enumerate(((chip_x, chip_y, 0), (chip_y, chip_x, PIECE // 2)))]
 
     def h_forward(s):
-        return remote(hbuf.at[s], hbuf.at[s], fw_send.at[s // 2], h_sem.at[s], partner)
+        return remote(hbuf.at[s], hbuf.at[s], fw_send.at[s // 2], h_fwd.at[s // 2], partner)
 
     def stats_sends(s):
         return [remote(st_send.at[s], st_recv.at[s, me], st_ssem.at[s], st_rsem.at[s], (me + i) % (2 * CHIPS)) for i in range(1, 2 * CHIPS)]
@@ -128,20 +136,40 @@
         def _():
             pair_copy(u - 3).start()
 
+    def first_set(u):
+        return jnp.minimum(DIRECT + u + 2 * jnp.clip(u - 2, 0, 2), steps)
+
+    def h_ready(s, lo):
+        for i in range(lo, 3):
+            wait_bytes(hbuf.at[s, pl.ds(0, PIECE)], h_recv.at[i, s // 2])
+
     def h_stages(u):
-        @pl.when((u + 4 < steps) & (u % 2 == core))
-        def _():
-            for copy in h_sends((u + 4) // 2):
+        for i in range(3):
+            @pl.when((first_set(u) + i < first_set(u + 1)) & ((first_set(u) + i) % 2 == core))
+            def _():
+                for copy in h_sends((first_set(u) + i) // 2, False):
+                    copy.start()
+
+        @pl.when((u + 2 >= DIRECT) & (u + 2 < steps) & (u % 2 == core))
+        def _():
+            for i in range(2):
+                wait_bytes(hbuf.at[u + 2, pl.ds(0, PIECE)], h_recv.at[i, (u + 2) // 2])
+            for copy in h_relays(u + 2):
                 copy.start()
 
-        @pl.when((u + 1 < steps) & ((u + 1) % 2 == core))
-        def _():
-            wait_bytes(hbuf.at[u + 1], h_sem.at[u + 1])
+        @pl.when((u + 1 < DIRECT) & ((u + 1) % 2 == core))
+        def _():
+            h_ready(u + 1, 0)
             h_forward(u + 1).start()
 
+        @pl.when((u + 1 >= DIRECT) & (u + 1 < steps) & ((u + 1) % 2 == core))
+        def _():
+            h_ready(u + 1, 2)
+            h_forward(u + 1).start()
+
         @pl.when((u < steps) & (u % 2 != core))
         def _():
-            wait_bytes(hbuf.at[u], h_sem.at[u])
+            wait_bytes(hbuf.at[u], h_fwd.at[u // 2])
 
     def target_row(s):
         row = jnp.concatenate([tbuf[2 * j + s % 2, pl.ds(s // 2, 1), :] for j in range(CHIPS)], axis=1)
@@ -157,7 +185,7 @@
         lse_row = jnp.concatenate([lse[j:j + 1] for j in range(CHIPS)], axis=1)
         factor[...] = jnp.exp(runmax[s % 2] - lse_row) * inv_tokens
 
-    def chunks(u, fwd, bwd):
+    def chunks(u, fwd, bwd, late_dw=False):
         par = u % 2
         if fwd:
             h_f = hbuf.at[u]
@@ -174,7 +202,10 @@
                     dz_ref = dzs[c % 2]
                     ids = lax.broadcasted_iota(jnp.int32, (n, STEP_TOK), 0) + lo
                     hot = jnp.where(ids == t_b, inv_tokens, 0.0)
-                    dz_ref[:n] = (probs[par, lo:lo + n] * factor[c:c + 1] - hot).astype(jnp.bfloat16)
+                    dz = (probs[par, lo:lo + n] * factor[c:c + 1] - hot).astype(jnp.bfloat16)
+                    dz_ref[:n] = dz
+                    if late_dw:
+                        probs[par, lo:lo + n] = dz.astype(F32)
                     if n < CHUNK:
                         dz_ref[n:] = jnp.zeros((CHUNK - n, STEP_TOK), jnp.bfloat16)
                 if fwd:
@@ -189,7 +220,8 @@
                         dh_acc[par] = part
                     else:
                         dh_acc[par] += part
-                    dw_acc[lo:lo + n] += jnp.dot(dz_ref[:n], h_b[...], preferred_element_type=F32)
+                    if not late_dw:
+                        dw_acc[lo:lo + n] += jnp.dot(dz_ref[:n], h_b[...], preferred_element_type=F32)
                 if fwd:
                     z = zbufs[p % 2][:n]
                     new_m = jnp.max(z, axis=0, keepdims=True)
@@ -215,43 +247,56 @@
             for copy in stats_sends(u):
                 copy.start()
 
+    def late_chunks(s):
+        for c in range(n_chunks):
+            lo, n = c * CHUNK, chunk_rows(c)
+            dw_acc[lo:lo + n] += jnp.dot(probs[s % 2, lo:lo + n].astype(jnp.bfloat16), hbuf[s], preferred_element_type=F32)
+
     def prepare(u):
         reduce_stages(u)
         h_stages(u)
 
+    def own_piece(q):
+        return pltpu.make_async_copy(hid.at[pl.ds(pl.multiple_of(q * PIECE, PIECE), PIECE)], piece(2 * q + core, chip), h_own.at[q])
+
+    def start_piece(q, _):
+        own_piece(q).start()
+        return 0
+
+    def wait_piece(q, _):
+        own_piece(q).wait()
+        return 0
+
+    lax.fori_loop(0, steps // 2, start_piece, 0)
+    w_copy = pltpu.make_async_copy(w_in, w, w_sem)
+    w_copy.start()
     barrier = pltpu.get_barrier_semaphore()
     for i in range(1, 2 * CHIPS):
         pl.semaphore_signal(barrier, inc=1, device_id={"fsdp": (me + i) % (2 * CHIPS)}, device_id_type=pl.DeviceIdType.MESH)
+    lax.fori_loop(0, steps // 2, wait_piece, 0)
     pl.semaphore_wait(barrier, 2 * CHIPS - 1)
-
-    def own_piece(q, _):
-        s = 2 * q + core
-        pltpu.make_async_copy(hid.at[pl.ds(pl.multiple_of(q * PIECE, PIECE), PIECE)],
-                              hbuf.at[s, pl.ds(pl.multiple_of(chip * PIECE, PIECE), PIECE)], h_sem.at[s]).start()
-        return 0
-
-    lax.fori_loop(0, steps // 2, own_piece, 0)
-    for copy in h_sends(0):
+    for copy in h_sends(0, True):
         copy.start()
     pltpu.make_async_copy(tgt, tbuf.at[me], t_sem).start()
     t_copies = [remote(tgt, tbuf.at[me], t_send, t_sem, (me + i) % (2 * CHIPS)) for i in range(1, 2 * CHIPS)]
     for copy in t_copies:
         copy.start()
-    for copy in h_sends(1):
+    for copy in h_sends(1, True):
         copy.start()
 
+    dw_acc[...] = jnp.zeros_like(dw_acc)
+    tgt_sum[...] = jnp.zeros_like(tgt_sum)
+    lse_sum[...] = jnp.zeros_like(lse_sum)
+    w_copy.wait()
     for c in range(n_chunks):
         n = chunk_rows(c)
         wt[:, c * CHUNK:c * CHUNK + n] = w[c * CHUNK:c * CHUNK + n].T
     if last_rows < CHUNK:
         wt[:, vocab:] = jnp.zeros((width, n_chunks * CHUNK - vocab), jnp.bfloat16)
-    dw_acc[...] = jnp.zeros_like(dw_acc)
-    tgt_sum[...] = jnp.zeros_like(tgt_sum)
-    lse_sum[...] = jnp.zeros_like(lse_sum)
 
     @pl.when(core == 0)
     def _():
-        wait_bytes(hbuf.at[0], h_sem.at[0])
+        h_ready(0, 0)
         h_forward(0).start()
 
     wait_bytes(tbuf, t_sem)
@@ -270,7 +315,12 @@
     def bwd_step(u, _):
         prepare(u)
         finish_stats(u - 2)
-        chunks(u, False, True)
+        chunks(u, False, True, late_dw=True)
+        return 0
+
+    def late_step(u, _):
+        reduce_stages(u)
+        late_chunks(u - 4)
         return 0
 
     def tail_step(u, _):
@@ -286,22 +336,30 @@
     for i in range(1, 2 * CHIPS):
         remote(tt_send, tt_recv.at[me], tt_sem.at[0], tt_sem.at[1], (me + i) % (2 * CHIPS)).start()
     lax.fori_loop(steps, steps + 2, bwd_step, 0)
-    dw_copy = pltpu.make_async_copy(dw_acc, dw_out, dw_sem)
-    dw_copy.start()
+    lax.fori_loop(steps + 2, steps + 4, late_step, 0)
     wait_bytes(tt_recv, tt_sem.at[1])
     loss_out[0] = (jnp.sum(lse_sum[...]) - jnp.sum(tt_recv[...])) * inv_tokens
-    lax.fori_loop(steps + 2, steps + 6, tail_step, 0)
+    lax.fori_loop(steps + 4, steps + 6, tail_step, 0)
 
     wait_bytes(dh_out, out_sem)
-    dw_copy.wait()
     peers = 2 * CHIPS - 1
     wait_bytes(tbuf.at[:peers], t_send)
     wait_bytes(tt_recv.at[:peers], tt_sem.at[0])
 
     def drain_pieces(q, _):
-        for copy in h_sends(q):
-            copy.wait_send()
-        wait_bytes(hbuf.at[2 * q + core], fw_send.at[q])
+        for i in range(2):
+            wait_bytes(hbuf.at[0, pl.ds(0, PIECE)], h_send.at[i, q])
+
+        @pl.when(2 * q < DIRECT)
+        def _():
+            wait_bytes(hbuf.at[0, pl.ds(0, PIECE)], h_send.at[2, q])
+
+        @pl.when(2 * q >= DIRECT)
+        def _():
+            for i in range(2):
+                wait_bytes(hbuf.at[0, pl.ds(0, PIECE // 2)], h_send.at[3 + i, q])
+
+        wait_bytes(hbuf.at[0], fw_send.at[q])
         wait_bytes(out_stage.at[2 * q], out_send.at[q])
         return 0
 
@@ -328,11 +386,11 @@
         half = width // 2
         dma, bf16 = pltpu.SemaphoreType.DMA, jnp.bfloat16
         vmem = pl.BlockSpec(memory_space=pltpu.VMEM)
-        anyspace = pl.BlockSpec(memory_space=pl.ANY)
+        hbm = pl.BlockSpec(memory_space=pltpu.HBM)
         scratch = [
+            pltpu.VMEM((vocab, width), bf16),
             pltpu.VMEM((width, padded), bf16),
-            pltpu.VMEM((2, padded, STEP_TOK), F32),
-            pltpu.VMEM((vocab, width), F32),
+            pltpu.VMEM((2, vocab, STEP_TOK), F32),
             pltpu.VMEM((steps, STEP_TOK, width), bf16),
             pltpu.VMEM((groups, tok_loc // PIECE, PIECE), jnp.int32),
             pltpu.VMEM((CHUNK, STEP_TOK), F32), pltpu.VMEM((CHUNK, STEP_TOK), F32),
@@ -353,20 +411,21 @@
             pltpu.VMEM((2, half, PIECE), F32),
             pltpu.VMEM((2, half, PIECE), F32),
             pltpu.VMEM((steps, PIECE, half), F32),
-            dma((steps,)), dma((3, steps // 2)), dma((steps // 2,)),
+            dma(()), dma((steps // 2,)), dma((3, steps // 2)), dma((steps // 2,)),
+            dma((5, steps // 2)), dma((steps // 2,)),
             dma(()), dma(()),
             dma((steps,)), dma((steps,)),
             dma((2,)), dma((2, 2)), dma((2, 2)), dma((2, 2)),
-            dma(()), dma((steps // 2,)), dma(()),
+            dma(()), dma((steps // 2,)),
         ]
         flops = 6 * tok_loc * groups * vocab * width
         return pl.pallas_call(
             head_kernel,
-            out_shape=(jax.ShapeDtypeStruct((1,), F32), jax.ShapeDtypeStruct((tok_loc, width), F32), jax.ShapeDtypeStruct((vocab, width), F32)),
-            in_specs=[vmem, vmem, vmem],
-            out_specs=(pl.BlockSpec(memory_space=pltpu.SMEM), anyspace, anyspace),
+            out_shape=(jax.ShapeDtypeStruct((1,), F32), pltpu.VMEM((tok_loc, width), F32), pltpu.VMEM((vocab, width), F32)),
+            in_specs=[hbm, vmem, hbm],
+            out_specs=(pl.BlockSpec(memory_space=pltpu.SMEM), vmem, vmem),
             scratch_shapes=scratch,
-            compiler_params=pltpu.CompilerParams(collective_id=0, has_side_effects=True, vmem_limit_bytes=67_043_328),
+            compiler_params=pltpu.CompilerParams(collective_id=0, has_side_effects=True, vmem_limit_bytes=53_000_000),
             cost_estimate=pl.CostEstimate(flops=flops, bytes_accessed=20_000_000, transcendentals=tok_loc * groups * vocab),
         )(hidden, targets.reshape(tok_loc // PIECE, PIECE), weight)
 

time: 187 us -> 178 us (0.952)
  local copies, waits for them, and re-layouts: 10.7 us -> 4.66 us
  Pallas kernels: 173 us -> 171 us
    unnamed x2, local copies, waits for them, and re-layouts: 10.7 us -> 4.66 us
    pallas_call x1, Pallas kernels: 173 us -> 171 us  [local_head(): pl.pallas_call(head_kernel, out_shape=(jax.ShapeDtypeStruct((1,), F32), p...]
where the time goes in v3:
time: 178 us
  Pallas kernels  171 us (96%)
  local copies, waits for them, and re-layouts  4.66 us (3%)
  between operations  2.33 us (1%)
    pallas_call x1, Pallas kernels, local_head(): pl.pallas_call(head_kernel, out_shape=(jax.ShapeDtypeStruct((1,), F32), p...  171 us
    unnamed x2, local copies, waits for them, and re-layouts  4.66 us

profile of v3, /device:TPU:0, one launch (start us, length us, event | category | flops | bytes accessed | tf_op | source)
XLA Modules:
  0.0 178.1 jit_solution(11598133143005619085)
XLA Ops:
  0.6 171.1 %shard_map.58 = (f32[1]{0:T(128)}, f32[1024,512]{1,0:T(8,128)S(1)}, f32[4016,512]{1,0:T(8,128)S(1)}) custom-call(bf16[1024,512]{1,0:T(8,128)(2,1)} %hid.1, s32[8,128]{1,0:T(8,128)} %bitcast.1, bf16[4016,512]{1,0:T(8,128)(2,1)} %w_in.1), custom_call_target="tpu_custom_call" | custom-call | flops 101065949184 | bytes 20000000 | tf_op jit(solution)/shard_map/pallas_call | solution.py:422
  171.8 1.3 copy.9
  173.1 3.3 %copy.10 = f32[4016,512]{1,0:T(8,128)} copy(f32[4016,512]{1,0:T(8,128)S(1)} %get-tuple-element.5) | data formatting | bytes 16449536

commit v4 on v3

--- a/solution.py
+++ b/solution.py
@@ -10,6 +10,8 @@
 PIECE = 128
 CHIPS = 4
 STEP_TOK = PIECE * CHIPS
+TILE = 64
+SLOTS = 4
 DIRECT = 4
 CHUNK = 512
 F32 = jnp.float32
@@ -72,12 +74,12 @@
         return remote(dh_acc.at[s % 2, rows], pair_buf.at[s % 2], pair_sem.at[0, s % 2], pair_sem.at[1, s % 2], partner)
 
     def s1_copies(s):
-        sl = s % 2
+        sl = s % SLOTS
         return [remote(s1_buf.at[sl, block], r1_buf.at[sl, i], s1_sem.at[0, sl], s1_sem.at[1, sl], chip_1 * 2 + core)
                 for i, block in enumerate((chip_1, chip_d))]
 
     def s2_copy(s):
-        return remote(s2_buf.at[s % 2], r2_buf.at[s % 2], s2_sem.at[0, s % 2], s2_sem.at[1, s % 2], chip_2 * 2 + core)
+        return remote(s2_buf.at[s % SLOTS], r2_buf.at[s % SLOTS], s2_sem.at[0, s % SLOTS], s2_sem.at[1, s % SLOTS], chip_2 * 2 + core)
 
     def out_dst(s):
         return dh_out.at[pl.ds(pl.multiple_of(s // 2 * PIECE, PIECE), PIECE), pl.ds(pl.multiple_of(core * half, half), half)]
@@ -86,11 +88,12 @@
         return remote(out_stage.at[s], out_dst(s), out_send.at[s // 2], out_sem, partner)
 
     def reduce_stages(u):
-        @pl.when((u >= 6) & (u < steps + 6))
-        def _():
-            s = u - 6
-            wait_bytes(r2_buf.at[s % 2], s2_sem.at[1, s % 2])
-            out_stage[s] = (own_buf[s % 2] + r2_buf[s % 2]).T
+        @pl.when((u >= 8) & (u < steps + 8))
+        def _():
+            s = u - 8
+            sl = s % SLOTS
+            wait_bytes(r2_buf.at[sl], s2_sem.at[1, sl])
+            out_stage[s] = (own_buf[sl] + r2_buf[sl]).T
 
             @pl.when(s % 2 == core)
             def _():
@@ -100,13 +103,13 @@
             def _():
                 out_remote(s).start()
 
-        @pl.when((u >= 5) & (u < steps + 5))
-        def _():
-            s = u - 5
-            sl = s % 2
+        @pl.when((u >= 6) & (u < steps + 6))
+        def _():
+            s = u - 6
+            sl = s % SLOTS
             wait_bytes(r1_buf.at[sl], s1_sem.at[1, sl])
 
-            @pl.when(s >= 2)
+            @pl.when(s >= SLOTS)
             def _():
                 wait_bytes(s2_buf.at[sl], s2_sem.at[0, sl])
 
@@ -118,17 +121,18 @@
         def _():
             s = u - 4
             sl = s % 2
+            sl1 = s % SLOTS
             wait_bytes(pair_buf.at[sl], pair_sem.at[1, sl])
             wait_bytes(pair_buf.at[sl], pair_sem.at[0, sl])
 
-            @pl.when(s >= 2)
+            @pl.when(s >= SLOTS)
             def _():
-                wait_bytes(r1_buf.at[sl], s1_sem.at[0, sl])
+                wait_bytes(r1_buf.at[sl1], s1_sem.at[0, sl1])
 
             rows = pl.ds(pl.multiple_of(core * half, half), half)
             for j in range(CHIPS):
                 cols = pl.ds(j * PIECE, PIECE)
-                s1_buf[sl, j] = dh_acc[sl, rows, cols] + pair_buf[sl, :, cols]
+                s1_buf[sl1, j] = dh_acc[sl, rows, cols] + pair_buf[sl, :, cols]
             for copy in s1_copies(s):
                 copy.start()
 
@@ -170,6 +174,9 @@
         @pl.when((u < steps) & (u % 2 != core))
         def _():
             wait_bytes(hbuf.at[u], h_fwd.at[u // 2])
+
+    def row_ids(lo, n):
+        return jnp.concatenate([lax.broadcasted_iota(jnp.int32, (n, PIECE), 0) + lo] * CHIPS, axis=1)
 
     def target_row(s):
         row = jnp.concatenate([tbuf[2 * j + s % 2, pl.ds(s // 2, 1), :] for j in range(CHIPS)], axis=1)
@@ -194,22 +201,30 @@
             s = u - 2
             h_b = hbuf.at[s]
             t_b = target_row(s)
-        run_m = run_s = tacc = None
+        run_m = run_s = tacc = new_m = None
         for c in range(n_chunks + 1):
+            if c > 0 and fwd:
+                p, m = c - 1, new_m
             if c < n_chunks:
                 lo, n = c * CHUNK, chunk_rows(c)
                 if bwd:
                     dz_ref = dzs[c % 2]
-                    ids = lax.broadcasted_iota(jnp.int32, (n, STEP_TOK), 0) + lo
-                    hot = jnp.where(ids == t_b, inv_tokens, 0.0)
-                    dz = (probs[par, lo:lo + n] * factor[c:c + 1] - hot).astype(jnp.bfloat16)
-                    dz_ref[:n] = dz
-                    if late_dw:
-                        probs[par, lo:lo + n] = dz.astype(F32)
+                    for r in range(0, n, TILE):
+                        k = min(TILE, n - r)
+                        hot = jnp.where(row_ids(lo + r, k) == t_b, inv_tokens, 0.0)
+                        dz = (probs[par, lo + r:lo + r + k] * factor[c:c + 1] - hot).astype(jnp.bfloat16)
+                        dz_ref[r:r + k] = dz
+                        if late_dw:
+                            probs[par, lo + r:lo + r + k] = dz.astype(F32)
                     if n < CHUNK:
                         dz_ref[n:] = jnp.zeros((CHUNK - n, STEP_TOK), jnp.bfloat16)
                 if fwd:
-                    zbufs[c % 2][:n] = lax.dot_general(w[lo:lo + n], h_f[...], (((1,), (1,)), ((), ())), preferred_element_type=F32)
+                    z = lax.dot_general(w[lo:lo + n], h_f[...], (((1,), (1,)), ((), ())), preferred_element_type=F32)
+                    zbufs[c % 2][:n] = z
+                    new_m = jnp.max(z, axis=0, keepdims=True)
+                    if c > 0:
+                        new_m = jnp.maximum(new_m, m)
+                    runmax[par, c:c + 1] = new_m
             if c > 0:
                 p = c - 1
                 lo, n = p * CHUNK, chunk_rows(p)
@@ -223,20 +238,22 @@
                     if not late_dw:
                         dw_acc[lo:lo + n] += jnp.dot(dz_ref[:n], h_b[...], preferred_element_type=F32)
                 if fwd:
-                    z = zbufs[p % 2][:n]
-                    new_m = jnp.max(z, axis=0, keepdims=True)
+                    part = hit = None
+                    for r in range(0, n, TILE):
+                        k = min(TILE, n - r)
+                        z = zbufs[p % 2][r:r + k]
+                        e = jnp.exp(z - m)
+                        probs[par, lo + r:lo + r + k] = e
+                        e = jnp.sum(e.reshape(k // 8, 8, STEP_TOK), axis=0)
+                        t = jnp.sum(jnp.where(row_ids(lo + r, k) == t_f, z, 0.0).reshape(k // 8, 8, STEP_TOK), axis=0)
+                        part, hit = (e, t) if part is None else (part + e, hit + t)
                     if p > 0:
-                        new_m = jnp.maximum(new_m, run_m)
-                    e = jnp.exp(z - new_m)
-                    probs[par, lo:lo + n] = e
-                    part = jnp.sum(e, axis=0, keepdims=True)
-                    ids = lax.broadcasted_iota(jnp.int32, (n, STEP_TOK), 0) + lo
-                    hit = jnp.sum(jnp.where(ids == t_f, z, 0.0), axis=0, keepdims=True)
-                    if p > 0:
-                        part = run_s * jnp.exp(run_m - new_m) + part
+                        part = run_s * jnp.exp(run_m - m) + part
                         hit = tacc + hit
-                    run_m, run_s, tacc = new_m, part, hit
-                    runmax[par, p:p + 1] = new_m
+                    run_m, run_s, tacc = m, part, hit
+        if fwd:
+            run_s = jnp.sum(run_s, axis=0, keepdims=True)
+            tacc = jnp.sum(tacc, axis=0, keepdims=True)
         if fwd:
             for j in range(CHIPS):
                 cols = slice(j * PIECE, (j + 1) * PIECE)
@@ -339,7 +356,7 @@
     lax.fori_loop(steps + 2, steps + 4, late_step, 0)
     wait_bytes(tt_recv, tt_sem.at[1])
     loss_out[0] = (jnp.sum(lse_sum[...]) - jnp.sum(tt_recv[...])) * inv_tokens
-    lax.fori_loop(steps + 4, steps + 6, tail_step, 0)
+    lax.fori_loop(steps + 4, steps + 8, tail_step, 0)
 
     wait_bytes(dh_out, out_sem)
     peers = 2 * CHIPS - 1
@@ -369,7 +386,7 @@
 
     lax.fori_loop(0, steps // 2, drain_pieces, 0)
     lax.fori_loop(0, steps, drain_stats, 0)
-    for sl in range(2):
+    for sl in range(SLOTS):
         wait_bytes(r1_buf.at[sl], s1_sem.at[0, sl])
         wait_bytes(s2_buf.at[sl], s2_sem.at[0, sl])
 
@@ -405,17 +422,17 @@
             pltpu.VMEM((8, PIECE), F32),
             pltpu.VMEM((groups, 8, PIECE), F32),
             pltpu.VMEM((2, half, STEP_TOK), F32),
-            pltpu.VMEM((2, CHIPS, half, PIECE), F32),
-            pltpu.VMEM((2, 2, half, PIECE), F32),
-            pltpu.VMEM((2, half, PIECE), F32),
-            pltpu.VMEM((2, half, PIECE), F32),
-            pltpu.VMEM((2, half, PIECE), F32),
+            pltpu.VMEM((SLOTS, CHIPS, half, PIECE), F32),
+            pltpu.VMEM((SLOTS, 2, half, PIECE), F32),
+            pltpu.VMEM((SLOTS, half, PIECE), F32),
+            pltpu.VMEM((SLOTS, half, PIECE), F32),
+            pltpu.VMEM((SLOTS, half, PIECE), F32),
             pltpu.VMEM((steps, PIECE, half), F32),
             dma(()), dma((steps // 2,)), dma((3, steps // 2)), dma((steps // 2,)),
             dma((5, steps // 2)), dma((steps // 2,)),
             dma(()), dma(()),
             dma((steps,)), dma((steps,)),
-            dma((2,)), dma((2, 2)), dma((2, 2)), dma((2, 2)),
+            dma((2,)), dma((2, 2)), dma((2, SLOTS)), dma((2, SLOTS)),
             dma(()), dma((steps // 2,)),
         ]
         flops = 6 * tok_loc * groups * vocab * width
@@ -425,7 +442,7 @@
             in_specs=[hbm, vmem, hbm],
             out_specs=(pl.BlockSpec(memory_space=pltpu.SMEM), vmem, vmem),
             scratch_shapes=scratch,
-            compiler_params=pltpu.CompilerParams(collective_id=0, has_side_effects=True, vmem_limit_bytes=53_000_000),
+            compiler_params=pltpu.CompilerParams(collective_id=0, has_side_effects=True, vmem_limit_bytes=56_000_000),
             cost_estimate=pl.CostEstimate(flops=flops, bytes_accessed=20_000_000, transcendentals=tok_loc * groups * vocab),
         )(hidden, targets.reshape(tok_loc // PIECE, PIECE), weight)
 

time: 178 us -> 164 us (0.921)
  Pallas kernels: 171 us -> 157 us
    pallas_call x1, Pallas kernels: 171 us -> 157 us  [local_head(): pl.pallas_call(head_kernel, out_shape=(jax.ShapeDtypeStruct((1,), F32), p...]
where the time goes in v4:
time: 164 us
  Pallas kernels  157 us (96%)
  local copies, waits for them, and re-layouts  4.66 us (3%)
  between operations  2.33 us (1%)
    pallas_call x1, Pallas kernels, local_head(): pl.pallas_call(head_kernel, out_shape=(jax.ShapeDtypeStruct((1,), F32), p...  157 us
    unnamed x2, local copies, waits for them, and re-layouts  4.66 us

profile of v4, /device:TPU:0, one launch (start us, length us, event | category | flops | bytes accessed | tf_op | source)
XLA Modules:
  0.0 163.6 jit_solution(17529835544503016656)
XLA Ops:
  0.6 156.6 %shard_map.58 = (f32[1]{0:T(128)}, f32[1024,512]{1,0:T(8,128)S(1)}, f32[4016,512]{1,0:T(8,128)S(1)}) custom-call(bf16[1024,512]{1,0:T(8,128)(2,1)} %hid.1, s32[8,128]{1,0:T(8,128)} %bitcast.1, bf16[4016,512]{1,0:T(8,128)(2,1)} %w_in.1), custom_call_target="tpu_custom_call" | custom-call | flops 101065949184 | bytes 20000000 | tf_op jit(solution)/shard_map/pallas_call | solution.py:439
  157.3 1.3 copy.9
  158.6 3.3 %copy.10 = f32[4016,512]{1,0:T(8,128)} copy(f32[4016,512]{1,0:T(8,128)S(1)} %get-tuple-element.5) | data formatting | bytes 16449536

commit v5 on v4

--- a/solution.py
+++ b/solution.py
@@ -10,9 +10,10 @@
 PIECE = 128
 CHIPS = 4
 STEP_TOK = PIECE * CHIPS
+GROUP = 1
 TILE = 64
 SLOTS = 4
-DIRECT = 4
+DIRECT = 6
 CHUNK = 512
 F32 = jnp.float32
 
@@ -141,7 +142,7 @@
             pair_copy(u - 3).start()
 
     def first_set(u):
-        return jnp.minimum(DIRECT + u + 2 * jnp.clip(u - 2, 0, 2), steps)
+        return jnp.minimum(4 + u + 2 * jnp.clip(u - 2, 0, 2), steps)
 
     def h_ready(s, lo):
         for i in range(lo, 3):
@@ -151,14 +152,17 @@
         for i in range(3):
             @pl.when((first_set(u) + i < first_set(u + 1)) & ((first_set(u) + i) % 2 == core))
             def _():
-                for copy in h_sends((first_set(u) + i) // 2, False):
-                    copy.start()
-
-        @pl.when((u + 2 >= DIRECT) & (u + 2 < steps) & (u % 2 == core))
+                for j, copy in enumerate(h_sends((first_set(u) + i) // 2, True)):
+                    if j < 2:
+                        copy.start()
+                    else:
+                        pl.when(u < 2)(lambda copy=copy: copy.start())
+
+        @pl.when((u + 3 >= DIRECT) & (u + 3 < steps) & ((u + 3) % 2 == core))
         def _():
             for i in range(2):
-                wait_bytes(hbuf.at[u + 2, pl.ds(0, PIECE)], h_recv.at[i, (u + 2) // 2])
-            for copy in h_relays(u + 2):
+                wait_bytes(hbuf.at[u + 3, pl.ds(0, PIECE)], h_recv.at[i, (u + 3) // 2])
+            for copy in h_relays(u + 3):
                 copy.start()
 
         @pl.when((u + 1 < DIRECT) & ((u + 1) % 2 == core))
@@ -201,56 +205,59 @@
             s = u - 2
             h_b = hbuf.at[s]
             t_b = target_row(s)
-        run_m = run_s = tacc = new_m = None
+        run_m = run_s = new_m = m = None
+        tacc = jnp.zeros((8, STEP_TOK), F32)
         for c in range(n_chunks + 1):
+            m = new_m
+            if c < n_chunks and bwd:
+                lo, n = c * CHUNK, chunk_rows(c)
+                dz_ref, at = dzs[c // GROUP % 2], c % GROUP * CHUNK
+                for r in range(0, n, TILE):
+                    k = min(TILE, n - r)
+                    hot = jnp.where(row_ids(lo + r, k) == t_b, inv_tokens, 0.0)
+                    dz = probs[par, lo + r:lo + r + k] * factor[c:c + 1] - hot
+                    dz_ref[at + r:at + r + k] = dz.astype(jnp.bfloat16)
+                    if late_dw:
+                        probs[par, lo + r:lo + r + k] = dz
+                if n < CHUNK:
+                    dz_ref[at + n:at + CHUNK] = jnp.zeros((CHUNK - n, STEP_TOK), jnp.bfloat16)
+            if c < n_chunks and fwd:
+                lo, n = c * CHUNK, chunk_rows(c)
+                z = lax.dot_general(w[lo:lo + n], h_f[...], (((1,), (1,)), ((), ())), preferred_element_type=F32)
+                zbufs[c % 2][:n] = z
+                new_m = jnp.max(z, axis=0, keepdims=True)
+                if c > 0:
+                    new_m = jnp.maximum(new_m, m)
+                runmax[par, c:c + 1] = new_m
+            if c > 0 and bwd and (c % GROUP == 0 or c == n_chunks):
+                g = (c - 1) // GROUP
+                lo = g * GROUP * CHUNK
+                n = min(GROUP * CHUNK, vocab - lo)
+                k = -(-n // CHUNK) * CHUNK
+                dz_ref = dzs[g % 2]
+                part = jnp.dot(wt[:, lo:lo + k], dz_ref[:k], preferred_element_type=F32)
+                if g == 0:
+                    dh_acc[par] = part
+                else:
+                    dh_acc[par] += part
+                if not late_dw:
+                    dw_acc[lo:lo + n] += jnp.dot(dz_ref[:n], h_b[...], preferred_element_type=F32)
             if c > 0 and fwd:
-                p, m = c - 1, new_m
-            if c < n_chunks:
-                lo, n = c * CHUNK, chunk_rows(c)
-                if bwd:
-                    dz_ref = dzs[c % 2]
-                    for r in range(0, n, TILE):
-                        k = min(TILE, n - r)
-                        hot = jnp.where(row_ids(lo + r, k) == t_b, inv_tokens, 0.0)
-                        dz = (probs[par, lo + r:lo + r + k] * factor[c:c + 1] - hot).astype(jnp.bfloat16)
-                        dz_ref[r:r + k] = dz
-                        if late_dw:
-                            probs[par, lo + r:lo + r + k] = dz.astype(F32)
-                    if n < CHUNK:
-                        dz_ref[n:] = jnp.zeros((CHUNK - n, STEP_TOK), jnp.bfloat16)
-                if fwd:
-                    z = lax.dot_general(w[lo:lo + n], h_f[...], (((1,), (1,)), ((), ())), preferred_element_type=F32)
-                    zbufs[c % 2][:n] = z
-                    new_m = jnp.max(z, axis=0, keepdims=True)
-                    if c > 0:
-                        new_m = jnp.maximum(new_m, m)
-                    runmax[par, c:c + 1] = new_m
-            if c > 0:
                 p = c - 1
                 lo, n = p * CHUNK, chunk_rows(p)
-                if bwd:
-                    dz_ref = dzs[p % 2]
-                    part = jnp.dot(wt[:, lo:lo + CHUNK], dz_ref[...], preferred_element_type=F32)
-                    if p == 0:
-                        dh_acc[par] = part
-                    else:
-                        dh_acc[par] += part
-                    if not late_dw:
-                        dw_acc[lo:lo + n] += jnp.dot(dz_ref[:n], h_b[...], preferred_element_type=F32)
-                if fwd:
-                    part = hit = None
-                    for r in range(0, n, TILE):
-                        k = min(TILE, n - r)
-                        z = zbufs[p % 2][r:r + k]
-                        e = jnp.exp(z - m)
-                        probs[par, lo + r:lo + r + k] = e
-                        e = jnp.sum(e.reshape(k // 8, 8, STEP_TOK), axis=0)
-                        t = jnp.sum(jnp.where(row_ids(lo + r, k) == t_f, z, 0.0).reshape(k // 8, 8, STEP_TOK), axis=0)
-                        part, hit = (e, t) if part is None else (part + e, hit + t)
-                    if p > 0:
-                        part = run_s * jnp.exp(run_m - m) + part
-                        hit = tacc + hit
-                    run_m, run_s, tacc = m, part, hit
+                part = None
+                for r in range(0, n, TILE):
+                    k = min(TILE, n - r)
+                    z = zbufs[p % 2][r:r + k]
+                    e = jnp.exp(z - m)
+                    probs[par, lo + r:lo + r + k] = e
+                    e = jnp.sum(e.reshape(k // 8, 8, STEP_TOK), axis=0)
+                    part = e if part is None else part + e
+                    for i in range(0, k, 8):
+                        tacc = jnp.where(row_ids(lo + r + i, 8) == t_f, z[i:i + 8], tacc)
+                if p > 0:
+                    part = run_s * jnp.exp(run_m - m) + part
+                run_m, run_s = m, part
         if fwd:
             run_s = jnp.sum(run_s, axis=0, keepdims=True)
             tacc = jnp.sum(tacc, axis=0, keepdims=True)
@@ -411,7 +418,7 @@
             pltpu.VMEM((steps, STEP_TOK, width), bf16),
             pltpu.VMEM((groups, tok_loc // PIECE, PIECE), jnp.int32),
             pltpu.VMEM((CHUNK, STEP_TOK), F32), pltpu.VMEM((CHUNK, STEP_TOK), F32),
-            pltpu.VMEM((CHUNK, STEP_TOK), bf16), pltpu.VMEM((CHUNK, STEP_TOK), bf16),
+            pltpu.VMEM((GROUP * CHUNK, STEP_TOK), bf16), pltpu.VMEM((GROUP * CHUNK, STEP_TOK), bf16),
             pltpu.VMEM((2, width, STEP_TOK), F32),
             pltpu.VMEM((2, padded // CHUNK, STEP_TOK), F32),
             pltpu.VMEM((padded // CHUNK, STEP_TOK), F32),

time: 164 us -> 167 us (1.018)
  Pallas kernels: 157 us -> 159 us
    pallas_call x1, Pallas kernels: 157 us -> 159 us  [local_head(): pl.pallas_call(head_kernel, out_shape=(jax.ShapeDtypeStruct((1,), F32), p...]
where the time goes in v5:
time: 167 us; the launch traced here: 166 us
  Pallas kernels  159 us (95%)
  local copies, waits for them, and re-layouts  4.66 us (3%)
  between operations  2.33 us (1%)
    pallas_call x1, Pallas kernels, local_head(): pl.pallas_call(head_kernel, out_shape=(jax.ShapeDtypeStruct((1,), F32), p...  159 us
    unnamed x2, local copies, waits for them, and re-layouts  4.66 us

profile of v5, /device:TPU:0, one launch (start us, length us, event | category | flops | bytes accessed | tf_op | source)
XLA Modules:
  0.0 166.4 jit_solution(7396650524204100051)
XLA Ops:
  0.6 159.4 %shard_map.58 = (f32[1]{0:T(128)}, f32[1024,512]{1,0:T(8,128)S(1)}, f32[4016,512]{1,0:T(8,128)S(1)}) custom-call(bf16[1024,512]{1,0:T(8,128)(2,1)} %hid.1, s32[8,128]{1,0:T(8,128)} %bitcast.1, bf16[4016,512]{1,0:T(8,128)(2,1)} %w_in.1), custom_call_target="tpu_custom_call" | custom-call | flops 101065949184 | bytes 20000000 | tf_op jit(solution)/shard_map/pallas_call | solution.py:446
  160.0 1.3 copy.9
  161.4 3.3 %copy.10 = f32[4016,512]{1,0:T(8,128)} copy(f32[4016,512]{1,0:T(8,128)S(1)} %get-tuple-element.5) | data formatting | bytes 16449536

commit v6 on v5

--- a/solution.py
+++ b/solution.py
@@ -13,7 +13,7 @@
 GROUP = 1
 TILE = 64
 SLOTS = 4
-DIRECT = 6
+DIRECT = 4
 CHUNK = 512
 F32 = jnp.float32
 
@@ -142,7 +142,7 @@
             pair_copy(u - 3).start()
 
     def first_set(u):
-        return jnp.minimum(4 + u + 2 * jnp.clip(u - 2, 0, 2), steps)
+        return jnp.minimum(DIRECT + u + 2 * jnp.clip(u - 2, 0, 2), steps)
 
     def h_ready(s, lo):
         for i in range(lo, 3):
@@ -152,17 +152,14 @@
         for i in range(3):
             @pl.when((first_set(u) + i < first_set(u + 1)) & ((first_set(u) + i) % 2 == core))
             def _():
-                for j, copy in enumerate(h_sends((first_set(u) + i) // 2, True)):
-                    if j < 2:
-                        copy.start()
-                    else:
-                        pl.when(u < 2)(lambda copy=copy: copy.start())
-
-        @pl.when((u + 3 >= DIRECT) & (u + 3 < steps) & ((u + 3) % 2 == core))
+                for copy in h_sends((first_set(u) + i) // 2, False):
+                    copy.start()
+
+        @pl.when((u + 2 >= DIRECT) & (u + 2 < steps) & (u % 2 == core))
         def _():
             for i in range(2):
-                wait_bytes(hbuf.at[u + 3, pl.ds(0, PIECE)], h_recv.at[i, (u + 3) // 2])
-            for copy in h_relays(u + 3):
+                wait_bytes(hbuf.at[u + 2, pl.ds(0, PIECE)], h_recv.at[i, (u + 2) // 2])
+            for copy in h_relays(u + 2):
                 copy.start()
 
         @pl.when((u + 1 < DIRECT) & ((u + 1) % 2 == core))

time: 167 us -> 164 us (0.982)
  Pallas kernels: 159 us -> 157 us
    pallas_call x1, Pallas kernels: 159 us -> 157 us  [local_head(): pl.pallas_call(head_kernel, out_shape=(jax.ShapeDtypeStruct((1,), F32), p...]
where the time goes in v6:
time: 164 us
  Pallas kernels  157 us (96%)
  local copies, waits for them, and re-layouts  4.66 us (3%)
  between operations  2.33 us (1%)
    pallas_call x1, Pallas kernels, local_head(): pl.pallas_call(head_kernel, out_shape=(jax.ShapeDtypeStruct((1,), F32), p...  157 us
    unnamed x2, local copies, waits for them, and re-layouts  4.66 us

profile of v6, /device:TPU:0, one launch (start us, length us, event | category | flops | bytes accessed | tf_op | source)
XLA Modules:
  0.0 164.3 jit_solution(10722160110750484179)
XLA Ops:
  0.6 157.3 %shard_map.58 = (f32[1]{0:T(128)}, f32[1024,512]{1,0:T(8,128)S(1)}, f32[4016,512]{1,0:T(8,128)S(1)}) custom-call(bf16[1024,512]{1,0:T(8,128)(2,1)} %hid.1, s32[8,128]{1,0:T(8,128)} %bitcast.1, bf16[4016,512]{1,0:T(8,128)(2,1)} %w_in.1), custom_call_target="tpu_custom_call" | custom-call | flops 101065949184 | bytes 20000000 | tf_op jit(solution)/shard_map/pallas_call | solution.py:443
  157.9 1.3 copy.9
  159.3 3.3 %copy.10 = f32[4016,512]{1,0:T(8,128)} copy(f32[4016,512]{1,0:T(8,128)S(1)} %get-tuple-element.5) | data formatting | bytes 16449536

commit v7 on v6

--- a/solution.py
+++ b/solution.py
@@ -88,58 +88,52 @@
     def out_remote(s):
         return remote(out_stage.at[s], out_dst(s), out_send.at[s // 2], out_sem, partner)
 
+    def finish_block(s):
+        sl = s % SLOTS
+        wait_bytes(r2_buf.at[sl], s2_sem.at[1, sl])
+        out_stage[s] = (own_buf[sl] + r2_buf[sl]).T
+
+        @pl.when(s % 2 == core)
+        def _():
+            pltpu.make_async_copy(out_stage.at[s], out_dst(s), out_sem).start()
+
+        @pl.when(s % 2 != core)
+        def _():
+            out_remote(s).start()
+
+    def second_stage(s):
+        sl = s % SLOTS
+        wait_bytes(r1_buf.at[sl], s1_sem.at[1, sl])
+
+        @pl.when(s >= SLOTS)
+        def _():
+            wait_bytes(s2_buf.at[sl], s2_sem.at[0, sl])
+
+        s2_buf[sl] = s1_buf[sl, chip_2] + r1_buf[sl, 1]
+        own_buf[sl] = s1_buf[sl, chip] + r1_buf[sl, 0]
+        s2_copy(s).start()
+
+    def first_stage(s):
+        sl, sl1 = s % 2, s % SLOTS
+        wait_bytes(pair_buf.at[sl], pair_sem.at[1, sl])
+        wait_bytes(pair_buf.at[sl], pair_sem.at[0, sl])
+
+        @pl.when(s >= SLOTS)
+        def _():
+            wait_bytes(r1_buf.at[sl1], s1_sem.at[0, sl1])
+
+        rows = pl.ds(pl.multiple_of(core * half, half), half)
+        for j in range(CHIPS):
+            cols = pl.ds(j * PIECE, PIECE)
+            s1_buf[sl1, j] = dh_acc[sl, rows, cols] + pair_buf[sl, :, cols]
+        for copy in s1_copies(s):
+            copy.start()
+
     def reduce_stages(u):
-        @pl.when((u >= 8) & (u < steps + 8))
-        def _():
-            s = u - 8
-            sl = s % SLOTS
-            wait_bytes(r2_buf.at[sl], s2_sem.at[1, sl])
-            out_stage[s] = (own_buf[sl] + r2_buf[sl]).T
-
-            @pl.when(s % 2 == core)
-            def _():
-                pltpu.make_async_copy(out_stage.at[s], out_dst(s), out_sem).start()
-
-            @pl.when(s % 2 != core)
-            def _():
-                out_remote(s).start()
-
-        @pl.when((u >= 6) & (u < steps + 6))
-        def _():
-            s = u - 6
-            sl = s % SLOTS
-            wait_bytes(r1_buf.at[sl], s1_sem.at[1, sl])
-
-            @pl.when(s >= SLOTS)
-            def _():
-                wait_bytes(s2_buf.at[sl], s2_sem.at[0, sl])
-
-            s2_buf[sl] = s1_buf[sl, chip_2] + r1_buf[sl, 1]
-            own_buf[sl] = s1_buf[sl, chip] + r1_buf[sl, 0]
-            s2_copy(s).start()
-
-        @pl.when((u >= 4) & (u < steps + 4))
-        def _():
-            s = u - 4
-            sl = s % 2
-            sl1 = s % SLOTS
-            wait_bytes(pair_buf.at[sl], pair_sem.at[1, sl])
-            wait_bytes(pair_buf.at[sl], pair_sem.at[0, sl])
-
-            @pl.when(s >= SLOTS)
-            def _():
-                wait_bytes(r1_buf.at[sl1], s1_sem.at[0, sl1])
-
-            rows = pl.ds(pl.multiple_of(core * half, half), half)
-            for j in range(CHIPS):
-                cols = pl.ds(j * PIECE, PIECE)
-                s1_buf[sl1, j] = dh_acc[sl, rows, cols] + pair_buf[sl, :, cols]
-            for copy in s1_copies(s):
-                copy.start()
-
-        @pl.when((u >= 3) & (u < steps + 3))
-        def _():
-            pair_copy(u - 3).start()
+        pl.when(u >= 8)(lambda: finish_block(u - 8))
+        pl.when(u >= 6)(lambda: second_stage(u - 6))
+        pl.when(u >= 4)(lambda: first_stage(u - 4))
+        pl.when(u >= 3)(lambda: pair_copy(u - 3).start())
 
     def first_set(u):
         return jnp.minimum(DIRECT + u + 2 * jnp.clip(u - 2, 0, 2), steps)
@@ -172,7 +166,7 @@
             h_ready(u + 1, 2)
             h_forward(u + 1).start()
 
-        @pl.when((u < steps) & (u % 2 != core))
+        @pl.when((u > 0) & (u < steps) & (u % 2 != core))
         def _():
             wait_bytes(hbuf.at[u], h_fwd.at[u // 2])
 
@@ -268,8 +262,8 @@
             for copy in stats_sends(u):
                 copy.start()
 
-    def late_chunks(s):
-        for c in range(n_chunks):
+    def late_chunks(s, which):
+        for c in which:
             lo, n = c * CHUNK, chunk_rows(c)
             dw_acc[lo:lo + n] += jnp.dot(probs[s % 2, lo:lo + n].astype(jnp.bfloat16), hbuf[s], preferred_element_type=F32)
 
@@ -296,13 +290,17 @@
         pl.semaphore_signal(barrier, inc=1, device_id={"fsdp": (me + i) % (2 * CHIPS)}, device_id_type=pl.DeviceIdType.MESH)
     lax.fori_loop(0, steps // 2, wait_piece, 0)
     pl.semaphore_wait(barrier, 2 * CHIPS - 1)
-    for copy in h_sends(0, True):
-        copy.start()
+
+    def send_set(q, of_core):
+        @pl.when(core == of_core)
+        def _():
+            for copy in h_sends(q, True):
+                copy.start()
+
+    send_set(0, 0)
     pltpu.make_async_copy(tgt, tbuf.at[me], t_sem).start()
     t_copies = [remote(tgt, tbuf.at[me], t_send, t_sem, (me + i) % (2 * CHIPS)) for i in range(1, 2 * CHIPS)]
     for copy in t_copies:
-        copy.start()
-    for copy in h_sends(1, True):
         copy.start()
 
     dw_acc[...] = jnp.zeros_like(dw_acc)
@@ -315,11 +313,20 @@
     if last_rows < CHUNK:
         wt[:, vocab:] = jnp.zeros((width, n_chunks * CHUNK - vocab), jnp.bfloat16)
 
+    send_set(0, 1)
+
     @pl.when(core == 0)
     def _():
         h_ready(0, 0)
         h_forward(0).start()
 
+    @pl.when(core == 1)
+    def _():
+        wait_bytes(hbuf.at[0], h_fwd.at[0])
+
+    for copy in h_sends(1, True):
+        copy.start()
+
     wait_bytes(tbuf, t_sem)
 
     def fwd_step(u, _):
@@ -337,15 +344,6 @@
         prepare(u)
         finish_stats(u - 2)
         chunks(u, False, True, late_dw=True)
-        return 0
-
-    def late_step(u, _):
-        reduce_stages(u)
-        late_chunks(u - 4)
-        return 0
-
-    def tail_step(u, _):
-        reduce_stages(u)
         return 0
 
     lax.fori_loop(0, 2, fwd_step, 0)
@@ -357,10 +355,23 @@
     for i in range(1, 2 * CHIPS):
         remote(tt_send, tt_recv.at[me], tt_sem.at[0], tt_sem.at[1], (me + i) % (2 * CHIPS)).start()
     lax.fori_loop(steps, steps + 2, bwd_step, 0)
-    lax.fori_loop(steps + 2, steps + 4, late_step, 0)
+    mid = n_chunks // 2
+    reduce_stages(jnp.int32(steps + 2))
+    late_chunks(steps - 2, range(mid))
+    finish_block(steps - 5)
+    second_stage(steps - 3)
+    first_stage(steps - 1)
+    late_chunks(steps - 2, range(mid, n_chunks))
+    late_chunks(steps - 1, range(mid))
+    finish_block(steps - 4)
+    second_stage(steps - 2)
+    late_chunks(steps - 1, range(mid, n_chunks))
     wait_bytes(tt_recv, tt_sem.at[1])
     loss_out[0] = (jnp.sum(lse_sum[...]) - jnp.sum(tt_recv[...])) * inv_tokens
-    lax.fori_loop(steps + 4, steps + 8, tail_step, 0)
+    finish_block(steps - 3)
+    second_stage(steps - 1)
+    finish_block(steps - 2)
+    finish_block(steps - 1)
 
     wait_bytes(dh_out, out_sem)
     peers = 2 * CHIPS - 1

time: 164 us -> 166 us (1.012)
  no operation moved by 1% of the time
where the time goes in v7:
time: 166 us; the launch traced here: 165 us
  Pallas kernels  158 us (95%)
  local copies, waits for them, and re-layouts  4.66 us (3%)
  between operations  2.33 us (1%)
    pallas_call x1, Pallas kernels, local_head(): pl.pallas_call(head_kernel, out_shape=(jax.ShapeDtypeStruct((1,), F32), p...  158 us
    unnamed x2, local copies, waits for them, and re-layouts  4.66 us

profile of v7, /device:TPU:0, one launch (start us, length us, event | category | flops | bytes accessed | tf_op | source)
XLA Modules:
  0.0 165.4 jit_solution(3627112480365831235)
XLA Ops:
  0.6 158.4 %shard_map.58 = (f32[1]{0:T(128)}, f32[1024,512]{1,0:T(8,128)S(1)}, f32[4016,512]{1,0:T(8,128)S(1)}) custom-call(bf16[1024,512]{1,0:T(8,128)(2,1)} %hid.1, s32[8,128]{1,0:T(8,128)} %bitcast.1, bf16[4016,512]{1,0:T(8,128)(2,1)} %w_in.1), custom_call_target="tpu_custom_call" | custom-call | flops 101065949184 | bytes 20000000 | tf_op jit(solution)/shard_map/pallas_call | solution.py:454
  159.0 1.3 copy.9
  160.3 3.3 %copy.10 = f32[4016,512]{1,0:T(8,128)} copy(f32[4016,512]{1,0:T(8,128)S(1)} %get-tuple-element.5) | data formatting | bytes 16449536

commit v8 on v7

--- a/solution.py
+++ b/solution.py
@@ -183,7 +183,7 @@
         m, e = stats[:, :CHIPS], stats[:, CHIPS:]
         top = jnp.max(m, axis=0)
         lse = top + jnp.log(jnp.sum(e * jnp.exp(m - top[None]), axis=0))
-        lse_sum[...] += lse
+        lse_sum[:CHIPS] += lse
         lse_row = jnp.concatenate([lse[j:j + 1] for j in range(CHIPS)], axis=1)
         factor[...] = jnp.exp(runmax[s % 2] - lse_row) * inv_tokens
 
@@ -251,7 +251,6 @@
                 run_m, run_s = m, part
         if fwd:
             run_s = jnp.sum(run_s, axis=0, keepdims=True)
-            tacc = jnp.sum(tacc, axis=0, keepdims=True)
         if fwd:
             for j in range(CHIPS):
                 cols = slice(j * PIECE, (j + 1) * PIECE)
@@ -348,12 +347,12 @@
 
     lax.fori_loop(0, 2, fwd_step, 0)
     lax.fori_loop(2, steps, both_step, 0)
-    row = tgt_sum[...]
+    row = jnp.sum(tgt_sum[...], axis=0, keepdims=True)
     tile = jnp.concatenate([row[:, j * PIECE:(j + 1) * PIECE] for j in range(CHIPS)] + [jnp.zeros((8 - CHIPS, PIECE), F32)], axis=0)
-    tt_send[...] = tile
-    pltpu.make_async_copy(tt_send, tt_recv.at[me], tt_sem.at[1]).start()
+    tt_send[:8] = tile
+    pltpu.make_async_copy(tt_send.at[:8], tt_recv.at[me], tt_sem.at[1]).start()
     for i in range(1, 2 * CHIPS):
-        remote(tt_send, tt_recv.at[me], tt_sem.at[0], tt_sem.at[1], (me + i) % (2 * CHIPS)).start()
+        remote(tt_send.at[:8], tt_recv.at[me], tt_sem.at[0], tt_sem.at[1], (me + i) % (2 * CHIPS)).start()
     lax.fori_loop(steps, steps + 2, bwd_step, 0)
     mid = n_chunks // 2
     reduce_stages(jnp.int32(steps + 2))
@@ -430,11 +429,11 @@
             pltpu.VMEM((2, width, STEP_TOK), F32),
             pltpu.VMEM((2, padded // CHUNK, STEP_TOK), F32),
             pltpu.VMEM((padded // CHUNK, STEP_TOK), F32),
-            pltpu.VMEM((1, STEP_TOK), F32),
-            pltpu.VMEM((CHIPS, PIECE), F32),
+            pltpu.VMEM((8, STEP_TOK), F32),
+            pltpu.VMEM((32, PIECE), F32),
             pltpu.VMEM((steps, 8, PIECE), F32),
             pltpu.VMEM((steps, groups, 8, PIECE), F32),
-            pltpu.VMEM((8, PIECE), F32),
+            pltpu.VMEM((32, PIECE), F32),
             pltpu.VMEM((groups, 8, PIECE), F32),
             pltpu.VMEM((2, half, STEP_TOK), F32),
             pltpu.VMEM((SLOTS, CHIPS, half, PIECE), F32),
@@ -454,7 +453,7 @@
         return pl.pallas_call(
             head_kernel,
             out_shape=(jax.ShapeDtypeStruct((1,), F32), pltpu.VMEM((tok_loc, width), F32), pltpu.VMEM((vocab, width), F32)),
-            in_specs=[hbm, vmem, hbm],
+            in_specs=[hbm, hbm, hbm],
             out_specs=(pl.BlockSpec(memory_space=pltpu.SMEM), vmem, vmem),
             scratch_shapes=scratch,
             compiler_params=pltpu.CompilerParams(collective_id=0, has_side_effects=True, vmem_limit_bytes=56_000_000),

time: 166 us -> 164 us (0.988)
  no operation moved by 1% of the time
where the time goes in v8:
time: 164 us
  Pallas kernels  157 us (96%)
  local copies, waits for them, and re-layouts  4.66 us (3%)
  between operations  2.33 us (1%)
    pallas_call x1, Pallas kernels, local_head(): pl.pallas_call(head_kernel, out_shape=(jax.ShapeDtypeStruct((1,), F32), p...  157 us
    unnamed x2, local copies, waits for them, and re-layouts  4.66 us

profile of v8, /device:TPU:0, one launch (start us, length us, event | category | flops | bytes accessed | tf_op | source)
XLA Modules:
  0.0 164.3 jit_solution(6610096778549175870)
XLA Ops:
  0.6 157.3 %shard_map.58 = (f32[1]{0:T(128)}, f32[1024,512]{1,0:T(8,128)S(1)}, f32[4016,512]{1,0:T(8,128)S(1)}) custom-call(bf16[1024,512]{1,0:T(8,128)(2,1)} %hid.1, s32[8,128]{1,0:T(8,128)} %bitcast.1, bf16[4016,512]{1,0:T(8,128)(2,1)} %w_in.1), custom_call_target="tpu_custom_call" | custom-call | flops 101065949184 | bytes 20000000 | tf_op jit(solution)/shard_map/pallas_call | solution.py:453
  158.0 1.3 copy.9
  159.3 3.3 %copy.10 = f32[4016,512]{1,0:T(8,128)} copy(f32[4016,512]{1,0:T(8,128)S(1)} %get-tuple-element.5) | data formatting | bytes 16449536

commit v9 on v8

--- a/solution.py
+++ b/solution.py
@@ -166,7 +166,7 @@
             h_ready(u + 1, 2)
             h_forward(u + 1).start()
 
-        @pl.when((u > 0) & (u < steps) & (u % 2 != core))
+        @pl.when((u < steps) & (u % 2 != core))
         def _():
             wait_bytes(hbuf.at[u], h_fwd.at[u // 2])
 
@@ -289,17 +289,13 @@
         pl.semaphore_signal(barrier, inc=1, device_id={"fsdp": (me + i) % (2 * CHIPS)}, device_id_type=pl.DeviceIdType.MESH)
     lax.fori_loop(0, steps // 2, wait_piece, 0)
     pl.semaphore_wait(barrier, 2 * CHIPS - 1)
-
-    def send_set(q, of_core):
-        @pl.when(core == of_core)
-        def _():
-            for copy in h_sends(q, True):
-                copy.start()
-
-    send_set(0, 0)
+    for copy in h_sends(0, True):
+        copy.start()
     pltpu.make_async_copy(tgt, tbuf.at[me], t_sem).start()
     t_copies = [remote(tgt, tbuf.at[me], t_send, t_sem, (me + i) % (2 * CHIPS)) for i in range(1, 2 * CHIPS)]
     for copy in t_copies:
+        copy.start()
+    for copy in h_sends(1, True):
         copy.start()
 
     dw_acc[...] = jnp.zeros_like(dw_acc)
@@ -312,19 +308,11 @@
     if last_rows < CHUNK:
         wt[:, vocab:] = jnp.zeros((width, n_chunks * CHUNK - vocab), jnp.bfloat16)
 
-    send_set(0, 1)
-
     @pl.when(core == 0)
     def _():
         h_ready(0, 0)
         h_forward(0).start()
 
-    @pl.when(core == 1)
-    def _():
-        wait_bytes(hbuf.at[0], h_fwd.at[0])
-
-    for copy in h_sends(1, True):
-        copy.start()
 
     wait_bytes(tbuf, t_sem)
 

time: 164 us -> 164 us (level)
  no operation moved by 1% of the time
where the time goes in v9:
time: 164 us; the launch traced here: 163 us
  Pallas kernels  157 us (96%)
  local copies, waits for them, and re-layouts  4.66 us (3%)
  between operations  2.33 us (1%)
    pallas_call x1, Pallas kernels, local_head(): pl.pallas_call(head_kernel, out_shape=(jax.ShapeDtypeStruct((1,), F32), p...  157 us
    unnamed x2, local copies, waits for them, and re-layouts  4.66 us

profile of v9, /device:TPU:0, one launch (start us, length us, event | category | flops | bytes accessed | tf_op | source)
XLA Modules:
  0.0 163.5 jit_solution(16243202054440994386)
XLA Ops:
  0.6 156.5 %shard_map.58 = (f32[1]{0:T(128)}, f32[1024,512]{1,0:T(8,128)S(1)}, f32[4016,512]{1,0:T(8,128)S(1)}) custom-call(bf16[1024,512]{1,0:T(8,128)(2,1)} %hid.1, s32[8,128]{1,0:T(8,128)} %bitcast.1, bf16[4016,512]{1,0:T(8,128)(2,1)} %w_in.1), custom_call_target="tpu_custom_call" | custom-call | flops 101065949184 | bytes 20000000 | tf_op jit(solution)/shard_map/pallas_call | solution.py:441
  157.1 1.3 copy.9
  158.5 3.3 %copy.10 = f32[4016,512]{1,0:T(8,128)} copy(f32[4016,512]{1,0:T(8,128)S(1)} %get-tuple-element.5) | data formatting | bytes 16449536

commit v10 on v9

--- a/solution.py
+++ b/solution.py
@@ -10,7 +10,6 @@
 PIECE = 128
 CHIPS = 4
 STEP_TOK = PIECE * CHIPS
-GROUP = 1
 TILE = 64
 SLOTS = 4
 DIRECT = 4
@@ -18,7 +17,7 @@
 F32 = jnp.float32
 
 
-def head_kernel(hid, tgt, w_in, loss_out, dh_out, dw_out, w, wt, probs, hbuf, tbuf, zbuf_a, zbuf_b, dz_a, dz_b, dh_acc,
+def head_kernel(hid, tgt, w_in, loss_out, dh_out, dw_out, w, wt, probs, hbuf, tbuf, zbuf_a, zbuf_b, dz_a, dz_b, dz_c, dh_acc,
                 runmax, factor, tgt_sum, lse_sum, st_send, st_recv, tt_send, tt_recv, pair_buf, s1_buf, r1_buf, s2_buf, r2_buf,
                 own_buf, out_stage, w_sem, h_own, h_recv, h_fwd, h_send, fw_send, t_sem, t_send, st_rsem, st_ssem, tt_sem, pair_sem,
                 s1_sem, s2_sem, out_sem, out_send):
@@ -31,7 +30,7 @@
     last_rows = vocab - (n_chunks - 1) * CHUNK
     inv_tokens = 1.0 / tokens
     dw_acc = dw_out
-    zbufs, dzs = (zbuf_a, zbuf_b), (dz_a, dz_b)
+    zbufs, dzs = (zbuf_a, zbuf_b), (dz_a, dz_b, dz_c)
 
     me = lax.axis_index("fsdp")
     core, chip = me % 2, me // 2
@@ -196,22 +195,25 @@
             s = u - 2
             h_b = hbuf.at[s]
             t_b = target_row(s)
+        def dlogits(c):
+            lo, n = c * CHUNK, chunk_rows(c)
+            dz_ref = dzs[c % len(dzs)]
+            for r in range(0, n, TILE):
+                k = min(TILE, n - r)
+                hot = jnp.where(row_ids(lo + r, k) == t_b, inv_tokens, 0.0)
+                dz = probs[par, lo + r:lo + r + k] * factor[c:c + 1] - hot
+                dz_ref[r:r + k] = dz.astype(jnp.bfloat16)
+                if late_dw:
+                    probs[par, lo + r:lo + r + k] = dz
+            if n < CHUNK:
+                dz_ref[n:] = jnp.zeros((CHUNK - n, STEP_TOK), jnp.bfloat16)
+
         run_m = run_s = new_m = m = None
         tacc = jnp.zeros((8, STEP_TOK), F32)
+        if bwd:
+            dlogits(0)
         for c in range(n_chunks + 1):
             m = new_m
-            if c < n_chunks and bwd:
-                lo, n = c * CHUNK, chunk_rows(c)
-                dz_ref, at = dzs[c // GROUP % 2], c % GROUP * CHUNK
-                for r in range(0, n, TILE):
-                    k = min(TILE, n - r)
-                    hot = jnp.where(row_ids(lo + r, k) == t_b, inv_tokens, 0.0)
-                    dz = probs[par, lo + r:lo + r + k] * factor[c:c + 1] - hot
-                    dz_ref[at + r:at + r + k] = dz.astype(jnp.bfloat16)
-                    if late_dw:
-                        probs[par, lo + r:lo + r + k] = dz
-                if n < CHUNK:
-                    dz_ref[at + n:at + CHUNK] = jnp.zeros((CHUNK - n, STEP_TOK), jnp.bfloat16)
             if c < n_chunks and fwd:
                 lo, n = c * CHUNK, chunk_rows(c)
                 z = lax.dot_general(w[lo:lo + n], h_f[...], (((1,), (1,)), ((), ())), preferred_element_type=F32)
@@ -220,19 +222,18 @@
                 if c > 0:
                     new_m = jnp.maximum(new_m, m)
                 runmax[par, c:c + 1] = new_m
-            if c > 0 and bwd and (c % GROUP == 0 or c == n_chunks):
-                g = (c - 1) // GROUP
-                lo = g * GROUP * CHUNK
-                n = min(GROUP * CHUNK, vocab - lo)
-                k = -(-n // CHUNK) * CHUNK
-                dz_ref = dzs[g % 2]
-                part = jnp.dot(wt[:, lo:lo + k], dz_ref[:k], preferred_element_type=F32)
-                if g == 0:
+            if c + 1 < n_chunks and bwd:
+                dlogits(c + 1)
+            if c < n_chunks and bwd:
+                part = jnp.dot(wt[:, c * CHUNK:(c + 1) * CHUNK], dzs[c % len(dzs)][...], preferred_element_type=F32)
+                if c == 0:
                     dh_acc[par] = part
                 else:
                     dh_acc[par] += part
-                if not late_dw:
-                    dw_acc[lo:lo + n] += jnp.dot(dz_ref[:n], h_b[...], preferred_element_type=F32)
+            if c > 0 and bwd and not late_dw:
+                p = c - 1
+                lo, n = p * CHUNK, chunk_rows(p)
+                dw_acc[lo:lo + n] += jnp.dot(dzs[p % len(dzs)][:n], h_b[...], preferred_element_type=F32)
             if c > 0 and fwd:
                 p = c - 1
                 lo, n = p * CHUNK, chunk_rows(p)
@@ -413,7 +414,7 @@
             pltpu.VMEM((steps, STEP_TOK, width), bf16),
             pltpu.VMEM((groups, tok_loc // PIECE, PIECE), jnp.int32),
             pltpu.VMEM((CHUNK, STEP_TOK), F32), pltpu.VMEM((CHUNK, STEP_TOK), F32),
-            pltpu.VMEM((GROUP * CHUNK, STEP_TOK), bf16), pltpu.VMEM((GROUP * CHUNK, STEP_TOK), bf16),
+            pltpu.VMEM((CHUNK, STEP_TOK), bf16), pltpu.VMEM((CHUNK, STEP_TOK), bf16), pltpu.VMEM((CHUNK, STEP_TOK), bf16),
             pltpu.VMEM((2, width, STEP_TOK), F32),
             pltpu.VMEM((2, padded // CHUNK, STEP_TOK), F32),
             pltpu.VMEM((padded // CHUNK, STEP_TOK), F32),

time: 164 us -> 163 us (level)
  no operation moved by 1% of the time
where the time goes in v10:
time: 163 us
  Pallas kernels  156 us (96%)
  local copies, waits for them, and re-layouts  4.66 us (3%)
  between operations  2.33 us (1%)
    pallas_call x1, Pallas kernels, local_head(): pl.pallas_call(head_kernel, out_shape=(jax.ShapeDtypeStruct((1,), F32), p...  156 us
    unnamed x2, local copies, waits for them, and re-layouts  4.66 us

profile of v10, /device:TPU:0, one launch (start us, length us, event | category | flops | bytes accessed | tf_op | source)
XLA Modules:
  0.0 162.9 jit_solution(10382343225680924875)
XLA Ops:
  0.6 155.9 %shard_map.58 = (f32[1]{0:T(128)}, f32[1024,512]{1,0:T(8,128)S(1)}, f32[4016,512]{1,0:T(8,128)S(1)}) custom-call(bf16[1024,512]{1,0:T(8,128)(2,1)} %hid.1, s32[8,128]{1,0:T(8,128)} %bitcast.1, bf16[4016,512]{1,0:T(8,128)(2,1)} %w_in.1), custom_call_target="tpu_custom_call" | custom-call | flops 101065949184 | bytes 20000000 | tf_op jit(solution)/shard_map/pallas_call | solution.py:442
  156.6 1.3 copy.9
  157.9 3.3 %copy.10 = f32[4016,512]{1,0:T(8,128)} copy(f32[4016,512]{1,0:T(8,128)S(1)} %get-tuple-element.5) | data formatting | bytes 16449536

commit v11 on v10

--- a/solution.py
+++ b/solution.py
@@ -135,14 +135,14 @@
         pl.when(u >= 3)(lambda: pair_copy(u - 3).start())
 
     def first_set(u):
-        return jnp.minimum(DIRECT + u + 2 * jnp.clip(u - 2, 0, 2), steps)
+        return jnp.minimum(DIRECT + u + 3 * jnp.clip(u - 2, 0, 2), steps)
 
     def h_ready(s, lo):
         for i in range(lo, 3):
             wait_bytes(hbuf.at[s, pl.ds(0, PIECE)], h_recv.at[i, s // 2])
 
     def h_stages(u):
-        for i in range(3):
+        for i in range(4):
             @pl.when((first_set(u) + i < first_set(u + 1)) & ((first_set(u) + i) % 2 == core))
             def _():
                 for copy in h_sends((first_set(u) + i) // 2, False):

time: 163 us -> 163 us (level)
  no operation moved by 1% of the time
where the time goes in v11:
time: 163 us
  Pallas kernels  156 us (96%)
  local copies, waits for them, and re-layouts  4.66 us (3%)
  between operations  2.33 us (1%)
    pallas_call x1, Pallas kernels, local_head(): pl.pallas_call(head_kernel, out_shape=(jax.ShapeDtypeStruct((1,), F32), p...  156 us
    unnamed x2, local copies, waits for them, and re-layouts  4.66 us

profile of v11, /device:TPU:0, one launch (start us, length us, event | category | flops | bytes accessed | tf_op | source)
XLA Modules:
  0.0 163.2 jit_solution(3038596839183123445)
XLA Ops:
  0.6 156.2 %shard_map.58 = (f32[1]{0:T(128)}, f32[1024,512]{1,0:T(8,128)S(1)}, f32[4016,512]{1,0:T(8,128)S(1)}) custom-call(bf16[1024,512]{1,0:T(8,128)(2,1)} %hid.1, s32[8,128]{1,0:T(8,128)} %bitcast.1, bf16[4016,512]{1,0:T(8,128)(2,1)} %w_in.1), custom_call_target="tpu_custom_call" | custom-call | flops 101065949184 | bytes 20000000 | tf_op jit(solution)/shard_map/pallas_call | solution.py:442
  156.8 1.3 copy.9
  158.1 3.3 %copy.10 = f32[4016,512]{1,0:T(8,128)} copy(f32[4016,512]{1,0:T(8,128)S(1)} %get-tuple-element.5) | data formatting | bytes 16449536

commit v12 on v10

--- a/solution.py
+++ b/solution.py
@@ -10,7 +10,7 @@
 PIECE = 128
 CHIPS = 4
 STEP_TOK = PIECE * CHIPS
-TILE = 64
+TILE = 32
 SLOTS = 4
 DIRECT = 4
 CHUNK = 512

time: 163 us -> 163 us (level)
  no operation moved by 1% of the time
where the time goes in v12:
time: 163 us
  Pallas kernels  156 us (96%)
  local copies, waits for them, and re-layouts  4.66 us (3%)
  between operations  2.33 us (1%)
    pallas_call x1, Pallas kernels, local_head(): pl.pallas_call(head_kernel, out_shape=(jax.ShapeDtypeStruct((1,), F32), p...  156 us
    unnamed x2, local copies, waits for them, and re-layouts  4.66 us

profile of v12, /device:TPU:0, one launch (start us, length us, event | category | flops | bytes accessed | tf_op | source)
XLA Modules:
  0.0 162.8 jit_solution(17793293535425005665)
XLA Ops:
  0.6 155.9 %shard_map.58 = (f32[1]{0:T(128)}, f32[1024,512]{1,0:T(8,128)S(1)}, f32[4016,512]{1,0:T(8,128)S(1)}) custom-call(bf16[1024,512]{1,0:T(8,128)(2,1)} %hid.1, s32[8,128]{1,0:T(8,128)} %bitcast.1, bf16[4016,512]{1,0:T(8,128)(2,1)} %w_in.1), custom_call_target="tpu_custom_call" | custom-call | flops 101065949184 | bytes 20000000 | tf_op jit(solution)/shard_map/pallas_call | solution.py:442
  156.5 1.3 copy.9
  157.8 3.3 %copy.10 = f32[4016,512]{1,0:T(8,128)} copy(f32[4016,512]{1,0:T(8,128)S(1)} %get-tuple-element.5) | data formatting | bytes 16449536
